TPU v7x, 512 devices: a whole 4x4x16 slice. The times are simulated.
512 devices in a mesh: ctx: 128 (over x, z, core), kv: 4 (over y).
Axes of the slice: x: 4, y: 4, z: 16, core: 2. Of those that a mesh axis runs over, the one named last changes fastest.
Arguments:
- queries: bfloat16 [16384, 10752], P('ctx', 'kv'), may hold values from -64 to 64
- keys: bfloat16 [16384, 768], P('ctx', 'kv'), may hold values from -4 to 4
- values: bfloat16 [16384, 512], P('ctx', 'kv'), may hold values from -5 to 5
- key_weights: float32 [32, 768], P(None, 'kv'), may hold values from -1 to 1
- value_weights: float32 [32, 512], P(None, 'kv'), may hold values from -1 to 1
- picks: int32 [256, 16], P('ctx'), may hold values from -1 to 255, as said below
- gates: float32 [2, 16384, 56], P(None, 'ctx', 'kv'), may hold values from -6 to 6
Outputs:
- attended: bfloat16 [16384, 7168], P('ctx', 'kv')
Inputs may be any that keep to these rules, and one draw needn't show every extreme that they name: `picks`: row t's first entry is t. Every other entry is -1 or a block p with p // 2 < t // 2. No row names a block twice, and the 2 rows t with the same t // 2 together name at most one block p for each value of p // 2 other than their own.
All inputs are finite; a program needn't handle non-finite values.
Results may differ from a plain program's by a relative error of at most 0.0061.
Values may be sent and summed in bfloat16 or wider, within the bound.
A program may use at most 64 MiB of HBM per device.

v0:
```python
import jax
import jax.numpy as jnp
from jax import lax
from jax.sharding import Mesh
from jax.sharding import PartitionSpec as P

BLOCK = 32
STRIDE = 16
TILE = 64
PICKS = 16
CTX = ("ctx_0", "ctx_1", "ctx_2")


neg_large = -1e30


def passed_along(value, axis, by):
    peers = lax.axis_size(axis)
    pairs = [(i, i + by) for i in range(peers) if 0 <= i + by < peers]
    return lax.ppermute(value, axis, pairs)


def laid_out(tiles, dim):
    shape = list(tiles.shape[1:])
    shape[dim] *= tiles.shape[0]
    return jnp.moveaxis(tiles, 0, dim).reshape(shape)


def all_blocks(value, axes, order):
    tiles = value
    for k in order:
        tiles = lax.all_gather(tiles, axes[k])
    done = order[::-1]
    back = [done.index(k) for k in range(len(axes))]
    tiles = tiles.transpose(*back, *range(len(axes), tiles.ndim))
    return tiles.reshape(-1, *value.shape)


def whole_of(value, axes, order, dim):
    return laid_out(all_blocks(value, axes, order), dim)


def compress(rows_in, following, weights):
    count = rows_in.shape[0]
    width = rows_in.shape[1]
    joined = jnp.concatenate([rows_in, following], 0).astype(jnp.float32)
    starts = joined[:count].reshape(count // STRIDE, STRIDE, width)
    ends = joined[STRIDE:].reshape(count // STRIDE, STRIDE, width)
    both = jnp.concatenate([starts, ends], 1)
    mixed = jnp.einsum("bjd,jd->bd", both, weights, precision=lax.Precision.HIGHEST)
    return mixed.astype(jnp.bfloat16)


def local(queries, keys, values, key_weights, value_weights, picks, gates):
    row_count = queries.shape[0]
    key_width = keys.shape[1]
    value_width = values.shape[1]
    head_count = gates.shape[2]
    tile_count = row_count // TILE
    inv_root = key_width ** (-0.5)
    query_heads = queries.reshape(row_count, head_count, key_width)
    self_index = lax.axis_index(CTX)
    shard_count = lax.axis_size(CTX)
    leading = jnp.concatenate([keys[:STRIDE], values[:STRIDE]], 1)
    following = passed_along(leading, CTX, -1)
    comp_keys = compress(keys, following[:, :key_width], key_weights)
    comp_values = compress(values, following[:, key_width:], value_weights)
    position = self_index * row_count + jnp.arange(row_count, dtype=jnp.int32)

    def absorb_piece(carry, item):
        run_max, run_sum, run_out = carry
        frag_keys, frag_values, first = item
        scores = (
            jnp.einsum("rhd,bd->rhb", query_heads, frag_keys, preferred_element_type=jnp.float32)
            * inv_root
        )
        block_end = (first + jnp.arange(frag_keys.shape[0], dtype=jnp.int32)) * STRIDE + BLOCK - 1
        visible = (block_end[None, :] <= position[:, None])[:, None, :]
        new_max = jnp.maximum(run_max, jnp.max(jnp.where(visible, scores, neg_large), axis=2))
        weights = jnp.where(visible, jnp.exp(scores - new_max[..., None]), 0.0)
        factor = jnp.exp(run_max - new_max)
        new_sum = run_sum * factor + jnp.sum(weights, axis=2)
        added = jnp.einsum(
            "rhb,bd->rhd",
            weights.astype(jnp.bfloat16),
            frag_values,
            preferred_element_type=jnp.float32,
        )
        return ((new_max, new_sum, run_out * factor[..., None] + added), None)

    start_state = (
        jnp.full((row_count, head_count), neg_large, jnp.float32),
        jnp.zeros((row_count, head_count), jnp.float32),
        jnp.zeros((row_count, head_count, value_width), jnp.float32),
    )
    frag_keys = whole_of(comp_keys, CTX, (0, 1, 2), 0)
    frag_values = whole_of(comp_values, CTX, (0, 1, 2), 0)
    total = frag_keys.shape[0]
    sub_rows = 16
    for candidate in (256, 128, 64, 32):
        sub_rows = candidate
        break
    pieces = total // sub_rows
    firsts = jnp.arange(pieces, dtype=jnp.int32) * sub_rows
    items = (
        frag_keys.reshape(pieces, sub_rows, key_width),
        frag_values.reshape(pieces, sub_rows, value_width),
        firsts,
    )
    result, unused = lax.scan(absorb_piece, start_state, items)
    last_max, last_sum, last_out = result
    comp_result = last_out / jnp.maximum(last_sum, 1.0)[..., None]
    own_keys = keys.reshape(tile_count, TILE, key_width)
    own_values = values.reshape(tile_count, TILE, value_width)
    owners = jnp.arange(shard_count, dtype=jnp.int32)
    flat_picks = picks.reshape(-1)
    pick_owner = flat_picks // tile_count
    match = (
        (pick_owner[None, :] == owners[:, None])
        & (flat_picks[None, :] >= 0)
        & (owners[:, None] != self_index)
    )
    wanted = jnp.max(jnp.where(match, (flat_picks % tile_count)[None, :], -1), axis=1)
    requested = lax.all_to_all(
        wanted.reshape(shard_count, 1), CTX, split_axis=0, concat_axis=0, tiled=True
    )
    onehot = (requested == jnp.arange(tile_count, dtype=jnp.int32)[None, :]).astype(jnp.bfloat16)
    reply_keys = jnp.einsum(
        "nt,trd->nrd", onehot, own_keys, preferred_element_type=jnp.float32
    ).astype(jnp.bfloat16)
    reply_values = jnp.einsum(
        "nt,trd->nrd", onehot, own_values, preferred_element_type=jnp.float32
    ).astype(jnp.bfloat16)
    got_keys, got_values = (
        lax.all_to_all(reply_keys, CTX, split_axis=0, concat_axis=0, tiled=True),
        lax.all_to_all(reply_values, CTX, split_axis=0, concat_axis=0, tiled=True),
    )
    key_table = jnp.concatenate([got_keys, own_keys], 0)
    value_table = jnp.concatenate([got_values, own_values], 0)
    owner_grid = picks // tile_count
    lookup = jnp.where(
        picks < 0,
        0,
        jnp.where(owner_grid == self_index, shard_count + picks % tile_count, owner_grid),
    )
    query_tiles = query_heads.reshape(tile_count, TILE, head_count, key_width)
    query_pos = position.reshape(tile_count, TILE)

    def select_one(item):
        tile_queries, picked, index_row, row_pos = item
        key_set = key_table[index_row].reshape(PICKS * TILE, key_width)
        value_set = value_table[index_row].reshape(PICKS * TILE, value_width)
        scores = (
            jnp.einsum("rhd,kd->rhk", tile_queries, key_set, preferred_element_type=jnp.float32)
            * inv_root
        )
        safe = jnp.maximum(picked, 0)
        key_pos = (safe[:, None] * TILE + jnp.arange(TILE, dtype=jnp.int32)[None, :]).reshape(-1)
        live = jnp.repeat(picked >= 0, TILE)
        visible = (live[None, :] & (key_pos[None, :] <= row_pos[:, None]))[:, None, :]
        top_score = jnp.max(jnp.where(visible, scores, neg_large), axis=2, keepdims=True)
        weights = jnp.where(visible, jnp.exp(scores - top_score), 0.0)
        mass_sum = jnp.sum(weights, axis=2)
        summed = jnp.einsum(
            "rhk,kd->rhd",
            weights.astype(jnp.bfloat16),
            value_set,
            preferred_element_type=jnp.float32,
        )
        return summed / mass_sum[..., None]

    sel_result = lax.map(select_one, (query_tiles, picks, lookup, query_pos)).reshape(
        row_count, head_count, value_width
    )
    gating = jax.nn.sigmoid(gates)
    mixed = gating[0][..., None] * comp_result + gating[1][..., None] * sel_result
    return mixed.reshape(row_count, head_count * value_width).astype(jnp.bfloat16)


def solution(mesh):
    split = Mesh(
        mesh.devices.reshape(4, 16, 2, mesh.shape["kv"]), ("ctx_0", "ctx_1", "ctx_2", "kv")
    )
    in_specs = (
        P(CTX, "kv"),
        P(CTX, "kv"),
        P(CTX, "kv"),
        P(None, "kv"),
        P(None, "kv"),
        P(CTX, None),
        P(None, CTX, "kv"),
    )
    out_specs = P(CTX, "kv")
    return jax.shard_map(local, mesh=split, in_specs=in_specs, out_specs=out_specs, check_vma=False)
```

profile of v0, /device:TPU:1, one launch (start us, length us, event | category | flops | bytes accessed | tf_op | source)
XLA Modules:
  0.0 486.6 jit_solution(13359795091829008661)
XLA Ops:
  1.0 35.2 %all_to_all.19 = s32[128,1,1]{2,1,0:T(1,128)S(1)} all-to-all(s32[128,1,1]{2,1,0:T(1,128)S(1)} %copy.104), channel_id=1, replica_groups=mesh['ctx_0'=4,'ctx_1'=16,'ctx_2'=2,'kv'=4] {'ctx_0','ctx_1','ctx_2'}, dimensions={0} | all-to-all | bytes 1024 | tf_op jit(solution)/shard_map/all_to_all | solution.py:124
  36.3 2.3 reduce.2
  40.2 2.7 copy.109
  42.9 6.6 %all-to-all-start.2 = ((bf16[128,64,128]{2,1,0:T(8,128)(2,1)}), bf16[128,64,128]{2,1,0:T(8,128)(2,1)S(1)}, u32[]{:S(2)}, u32[]{:S(2)}) async-start(bf16[128,64,128]{2,1,0:T(8,128)(2,1)} %copy.109), calls=%async_computation.2 | async-start | bytes 4194304 | tf_op jit(solution)/shard_map/all_to_all | solution.py:136
  49.6 3.0 convolution_convert_fusion
  52.7 6.8 %copy.107 = bf16[128,64,192]{2,1,0:T(8,128)(2,1)} copy(bf16[128,64,192]{0,2,1:T(8,128)(2,1)} %convolution_convert_fusion) | data formatting | bytes 6291456 | tf_op jit(solution)/shard_map/convert_element_type | solution.py:130
  59.5 89.4 %all-to-all-done.2 = bf16[128,64,128]{2,1,0:T(8,128)(2,1)S(1)} async-done(((bf16[128,64,128]{2,1,0:T(8,128)(2,1)}), bf16[128,64,128]{2,1,0:T(8,128)(2,1)S(1)}, u32[]{:S(2)}, u32[]{:S(2)}) %all-to-all-start.2) | async-done | bytes 2097184 | tf_op jit(solution)/shard_map/all_to_all | solution.py:136
  150.1 9.1 %all-to-all-start.1 = ((bf16[128,64,192]{2,1,0:T(8,128)(2,1)}), bf16[128,64,192]{2,1,0:T(8,128)(2,1)}, u32[]{:S(2)}, u32[]{:S(2)}) async-start(bf16[128,64,192]{2,1,0:T(8,128)(2,1)} %copy.107), calls=%async_computation.1 | async-start | bytes 8388608 | tf_op jit(solution)/shard_map/all_to_all | solution.py:135
  159.4 3.0 collective-permute-start
  170.6 167.7 %collective-permute-done = bf16[16,320]{1,0:T(8,128)(2,1)S(1)} collective-permute-done((bf16[16,320]{1,0:T(8,128)(2,1)S(1)}, bf16[16,320]{1,0:T(8,128)(2,1)S(1)}, u32[]{:S(2)}, u32[]{:S(2)}) %collective-permute-start) | collective-permute-done | bytes 10272 | tf_op jit(solution)/shard_map/ppermute | solution.py:20
  338.5 10.4 %all-gather = bf16[32,192]{1,0:T(8,128)(2,1)S(1)} all-gather(bf16[8,192]{1,0:T(8,128)(2,1)S(1)} %bitcast.170), channel_id=2, replica_groups=mesh['ctx_0'=4,'ctx_1'=16,'ctx_2'=2,'kv'=4] {'ctx_0'}, dimensions={0}, use_global_device_ids=true | all-gather | bytes 15360 | tf_op jit(solution)/shard_map/all_gather | solution.py:32
  348.8 24.9 %all-gather.1 = bf16[64,8,192]{2,1,0:T(8,128)(2,1)S(1)} all-gather(bf16[4,8,192]{2,1,0:T(8,128)(2,1)S(1)} %bitcast.167), channel_id=3, replica_groups=mesh['ctx_0'=4,'ctx_1'=16,'ctx_2'=2,'kv'=4] {'ctx_1'}, dimensions={0}, use_global_device_ids=true | all-gather | bytes 208896 | tf_op jit(solution)/shard_map/all_gather | solution.py:32
  373.8 10.3 %all-gather.2 = bf16[32,4,8,192]{3,2,1,0:T(8,128)(2,1)S(1)} all-gather(bf16[16,4,8,192]{3,2,1,0:T(8,128)(2,1)S(1)} %bitcast.157), channel_id=4, replica_groups=mesh['ctx_0'=4,'ctx_1'=16,'ctx_2'=2,'kv'=4] {'ctx_2'}, dimensions={0}, use_global_device_ids=true | all-gather | bytes 589824 | tf_op jit(solution)/shard_map/all_gather | solution.py:32
  384.4 8.1 %all-gather.3 = bf16[32,128]{1,0:T(8,128)(2,1)S(1)} all-gather(bf16[8,128]{1,0:T(8,128)(2,1)S(1)} %bitcast.172), channel_id=5, replica_groups=mesh['ctx_0'=4,'ctx_1'=16,'ctx_2'=2,'kv'=4] {'ctx_0'}, dimensions={0}, use_global_device_ids=true | all-gather | bytes 10240 | tf_op jit(solution)/shard_map/all_gather | solution.py:32
  392.6 20.3 %all-gather.4 = bf16[64,8,128]{2,1,0:T(8,128)(2,1)S(1)} all-gather(bf16[4,8,128]{2,1,0:T(8,128)(2,1)S(1)} %bitcast.169), channel_id=6, replica_groups=mesh['ctx_0'=4,'ctx_1'=16,'ctx_2'=2,'kv'=4] {'ctx_1'}, dimensions={0}, use_global_device_ids=true | all-gather | bytes 139264 | tf_op jit(solution)/shard_map/all_gather | solution.py:32
  412.9 11.2 %all-gather.5 = bf16[32,4,8,128]{3,2,1,0:T(8,128)(2,1)S(1)} all-gather(bf16[16,4,8,128]{3,2,1,0:T(8,128)(2,1)S(1)} %bitcast.160), channel_id=7, replica_groups=mesh['ctx_0'=4,'ctx_1'=16,'ctx_2'=2,'kv'=4] {'ctx_2'}, dimensions={0}, use_global_device_ids=true | all-gather | bytes 393216 | tf_op jit(solution)/shard_map/all_gather | solution.py:32
  424.2 24.3 %while.30 = (s32[]{:T(128)}, f32[128,14]{0,1:T(8,128)S(1)}, f32[128,14]{0,1:T(8,128)S(1)}, f32[128,14,128]{2,0,1:T(8,128)S(1)}, s32[4]{0:T(128)}, /*index=5*/bf1...) while((s32[]{:T(128)}, f32[128,14]{0,1:T(8,128)S(1)}, ...), condition=%wide.region_3.4_spmd.clone, body=%wide.region_0.3_spmd.clone.sunk | while | flops 299378304 | bytes 8443029 | solution.py:110
  448.5 3.2 pad_maximum_fusion.1
  451.7 4.9 %pad_maximum_fusion = bf16[130,64,192]{2,1,0:T(8,128)(2,1)} fusion(bf16[2,64,192]{2,1,0:T(8,128)(2,1)S(1)} %bitcast.156, bf16[128,64,192]{2,1,0:T(8,128)(2,1)} %all-to-all-done.1), kind=kLoop, calls=%fused_computation.67 | loop fusion | flops 1597440 | bytes 6389760 | tf_op jit(solution)/shard_map/concatenate | solution.py:138
  456.7 26.8 %while.29 = (s32[]{:T(128)}, f32[2,64,14,128]{3,1,0,2:T(8,128)}, s32[2,16]{1,0:T(2,128)S(1)}, s32[2,64]{1,0:T(2,128)S(1)}, bf16[2,64,14,192]{3,1,2,0:T(8,128)(2,...) while((s32[]{:T(128)}, f32[2,64,14,128]{3,1,0,2:T(8,128)}, ...), condition=%wide.region_8.9_spmd, body=%wide.region_5.8_spmd.sunk | while | flops 598463488 | bytes 40015396 | solution.py:172
  457.2 2.8 gather_fusion.1
  464.7 4.4 fusion.110
  470.6 2.8 gather_fusion.1
  478.1 4.4 fusion.110
  (143 shorter events, 52.2 us)
Async XLA Ops:
  40.2 9.4 %copy-start.6 = (bf16[128,192]{0,1:T(8,128)(2,1)S(1)}, bf16[128,192]{0,1:T(8,128)(2,1)}, u32[]{:S(2)}) copy-start(bf16[128,192]{0,1:T(8,128)(2,1)} %param.12) | copy-start | bytes 147460
  42.9 105.9 %all-to-all-start.2 = ((bf16[128,64,128]{2,1,0:T(8,128)(2,1)}), bf16[128,64,128]{2,1,0:T(8,128)(2,1)S(1)}, u32[]{:S(2)}, u32[]{:S(2)}) async-start(bf16[128,64,128]{2,1,0:T(8,128)(2,1)} %copy.109), calls=%async_computation.2 | async-start | bytes 4194304 | tf_op jit(solution)/shard_map/all_to_all | solution.py:136
  59.4 99.8 %copy-start.5 = (bf16[128,128]{1,0:T(8,128)(2,1)S(1)}, bf16[128,128]{1,0:T(8,128)(2,1)}, u32[]{:S(2)}) copy-start(bf16[128,128]{1,0:T(8,128)(2,1)} %param.13) | copy-start | bytes 98308
  59.5 103.6 %copy-start.12 = (s32[2,16]{1,0:T(2,128)S(1)}, s32[2,16]{1,0:T(2,128)}, u32[]{:S(2)}) copy-start(s32[2,16]{1,0:T(2,128)} %param.16) | copy-start | bytes 388
  59.5 104.1 %copy-start.11 = (f32[2,128,14]{1,0,2:T(2,128)S(1)}, f32[2,128,14]{1,0,2:T(2,128)}, u32[]{:S(2)}) copy-start(f32[2,128,14]{1,0,2:T(2,128)} %param.17) | copy-start | bytes 43012
  148.8 1.3 copy-start.2
  150.1 301.6 %all-to-all-start.1 = ((bf16[128,64,192]{2,1,0:T(8,128)(2,1)}), bf16[128,64,192]{2,1,0:T(8,128)(2,1)}, u32[]{:S(2)}, u32[]{:S(2)}) async-start(bf16[128,64,192]{2,1,0:T(8,128)(2,1)} %copy.107), calls=%async_computation.1 | async-start | bytes 8388608 | tf_op jit(solution)/shard_map/all_to_all | solution.py:135
  159.3 179.1 %copy-start.9 = (f32[32,192]{1,0:T(8,128)S(1)}, f32[32,192]{1,0:T(8,128)}, u32[]{:S(2)}) copy-start(f32[32,192]{1,0:T(8,128)} %param.14) | copy-start | bytes 73732
  159.4 179.0 %collective-permute-start = (bf16[16,320]{1,0:T(8,128)(2,1)S(1)}, bf16[16,320]{1,0:T(8,128)(2,1)S(1)}, u32[]{:S(2)}, u32[]{:S(2)}) collective-permute-start(bf16[16,320]{1,0:T(8,128)(2,1)S(1)} %pad_maximum_fusion.2), channel_id=1, source_target_pairs={{4,0},{8,4},{12,8},{16,12},{20,16},{24,20},{28,24},{32,28},{36,32}... | collective-permute-start | bytes 30728 | tf_op jit(solution)/shard_map/ppermute | solution.py:20
  167.1 217.3 %copy-start.10 = (f32[32,128]{1,0:T(8,128)S(1)}, f32[32,128]{1,0:T(8,128)}, u32[]{:S(2)}) copy-start(f32[32,128]{1,0:T(8,128)} %param.15) | copy-start | bytes 49156
  451.7 4.9 %copy-start.1 = (bf16[2,64,14,192]{3,1,2,0:T(8,128)(2,1)S(1)}, bf16[2,64,14,192]{3,1,2,0:T(8,128)(2,1)}, u32[]{:S(2)}) copy-start(bf16[2,64,14,192]{3,1,2,0:T(8,128)(2,1)} %copy.110) | copy-start | bytes 2064388
  451.7 4.9 %copy-start.13 = (s32[2,16]{1,0:T(2,128)S(1)}, s32[2,16]{1,0:T(2,128)}, u32[]{:S(2)}) copy-start(s32[2,16]{1,0:T(2,128)} %param.16) | copy-start | bytes 388
  451.7 4.9 %copy-start.14 = (s32[2,16]{1,0:T(2,128)S(1)}, s32[2,16]{1,0:T(2,128)}, u32[]{:S(2)}) copy-start(s32[2,16]{1,0:T(2,128)} %fusion.75) | copy-start | bytes 388
  451.7 4.9 %copy-start.15 = (s32[2,64]{1,0:T(2,128)S(1)}, s32[2,64]{1,0:T(2,128)}, u32[]{:S(2)}) copy-start(s32[2,64]{1,0:T(2,128)} %add_add_fusion) | copy-start | bytes 1540
  456.7 26.8 %copy-start.7 = (f32[128,14]{0,1:T(8,128)S(1)}, f32[128,14]{0,1:T(8,128)}, u32[]{:S(2)}) copy-start(f32[128,14]{0,1:T(8,128)} %get-tuple-element.398) | copy-start | bytes 21508
  456.7 26.8 %copy-start.8 = (f32[128,14]{0,1:T(8,128)S(1)}, f32[128,14]{0,1:T(8,128)}, u32[]{:S(2)}) copy-start(f32[128,14]{0,1:T(8,128)} %get-tuple-element.399) | copy-start | bytes 21508
  460.7 1.8 copy-start
  460.7 4.0 copy-start.3
  469.1 1.0 copy-start.4
  474.0 1.8 copy-start
  474.1 4.0 copy-start.3
  482.4 1.0 copy-start.4
where the time goes:
time: 488 us; the launch traced here: 487 us
  waiting for transfers between devices  257 us (53%)
  blocking collectives  121 us (25%)
  local copies, waits for them, and re-layouts  37.9 us (8%)
  matrix products  26.7 us (5%)
  other arithmetic  25 us (5%)
  starting transfers between devices  18.8 us (4%)
    ppermute x1, waiting for transfers between devices, passed_along(): return lax.ppermute(value, axis, pairs)  168 us
    all_to_all x1, waiting for transfers between devices, local(): lax.all_to_all(reply_values, CTX, split_axis=0, concat_axis=0, tiled=True)  89.4 us
    all_gather x6, blocking collectives, all_blocks(): tiles = lax.all_gather(tiles, axes[k])  85.3 us
    all_to_all x1, blocking collectives, local(): lax.all_to_all(wanted.reshape(shard_count, 1), CTX, split_axis=0, concat_...  35.2 us
  transfers between devices with their start and end apart: 3, of which 2 were waited for; matrix products, arithmetic and copies ran while one was open for 9% of the time, Pallas kernels for 0%

commit v1 on v0

v1 whole, which is shorter than its diff:
```python
import jax
import jax.numpy as jnp
from jax import lax
from jax.experimental import pallas as pl
from jax.experimental.pallas import tpu as pltpu
from jax.sharding import PartitionSpec as P

NX = 4
NZ = 16
HEADS = 14
PAIRS = HEADS // 2
DQK = 192
DV = 128
ROWS = 128
TILE = 64
PICKS = 16
CROWS = 32
KROWS = DQK + CROWS
LOW = -1e30
FLOOR = -1e29
COEF = DQK ** (-0.5) * 1.4426950408889634
F32 = jnp.float32
BF16 = jnp.bfloat16
MESH = pl.DeviceIdType.MESH


def gather_body(
    q_any, k_ref, v_ref, kw_ref, vw_ref, kb, vb, o_sc,
    q_vm, halo_k, halo_v, m_sc, cvext,
    q_sem, halo_s, halo_r, zk_s, zk_r, zv_s, zv_r, xv_s, xv_r, xk_s, xk_r, pk_s, pk_r, pv_s, pv_r,
):
    i = lax.axis_index("ctx")
    x = i // 32
    z = (i // 2) % NZ
    c = i % 2

    def at(xx, zz, cc):
        return (xx % NX) * 32 + (zz % NZ) * 2 + cc

    zside = (at(x, z + 1, c), at(x, z + NZ - 1, c))
    xside = (at(x + 1, z, c), at(x + NX - 1, z, c))
    partner = at(x, z, 1 - c)
    before = (i + 127) % 128
    after = (i + 1) % 128
    sends = []

    def remote(src, dst, ss, rs, target):
        return pltpu.make_async_remote_copy(
            src_ref=src, dst_ref=dst, send_sem=ss, recv_sem=rs,
            device_id={"ctx": target}, device_id_type=MESH,
        )

    def send(ref, ss, rs, target, dst=None):
        copy = remote(ref, ref if dst is None else dst, ss, rs, target)
        copy.start()
        sends.append(copy)

    def arrived(ref, ss, rs):
        remote(ref, ref, ss, rs, partner).wait_recv()

    barrier = pltpu.get_barrier_semaphore()
    for peer in (*zside, *xside, partner, before, after):
        pl.semaphore_signal(barrier, inc=1, device_id={"ctx": peer}, device_id_type=MESH)
    q_copy = pltpu.make_async_copy(q_any, q_vm, q_sem)
    q_copy.start()

    keys = k_ref[...].astype(F32)
    own_k = kb.at[c, z, x]
    own_k[pl.ds(0, 128), :] = jnp.transpose(keys[:, :128]).astype(BF16)
    own_k[pl.ds(128, 64), :] = jnp.transpose(keys[:, 128:]).astype(BF16)
    vb[c, z, x] = v_ref[...]
    pl.semaphore_wait(barrier, 7)

    send(k_ref.at[pl.ds(0, 16), :], halo_s.at[0], halo_r.at[0], before, halo_k)
    send(v_ref.at[pl.ds(0, 16), :], halo_s.at[1], halo_r.at[1], before, halo_v)

    def vz_send(zz, xx, step, col, dirs=(0, 1)):
        for d in dirs:
            send(vb.at[c, zz, xx], zv_s.at[d, step, col], zv_r.at[d, step, col], zside[d])

    for d in range(2):
        send(vb.at[c, z, x], xv_s.at[d], xv_r.at[d], xside[d])
    vz_send(z, x, 1, 0)

    o_sc[...] = jnp.zeros_like(o_sc)
    m_sc[...] = jnp.full_like(m_sc, FLOOR)
    cvext[:, 128:] = jnp.ones((128, 128), BF16)

    arrived(halo_k, halo_s.at[0], halo_r.at[0])
    arrived(halo_v, halo_s.at[1], halo_r.at[1])
    inside = (i != 127).astype(F32)

    def compress(rows, extra, weights):
        joined = jnp.concatenate([rows, extra.astype(F32) * inside], 0)
        parts = [
            jnp.sum(joined[16 * b:16 * b + 32] * weights, axis=0, keepdims=True) for b in range(8)
        ]
        return jnp.concatenate(parts, 0)

    ck = compress(keys, halo_k[...], kw_ref[...])
    cv = compress(v_ref[...].astype(F32), halo_v[...], vw_ref[...])
    zeros64 = jnp.zeros((8, 64), F32)
    ck_low = jnp.concatenate([ck[:, 128:], zeros64], 1)
    own_k[pl.ds(192, 16), :] = jnp.concatenate([ck[:, :128], ck_low], 0).astype(BF16)
    own_k[pl.ds(208, 16), :] = jnp.concatenate([cv, jnp.zeros((8, 128), F32)], 0).astype(BF16)

    def kx_send(zz):
        for d in range(2):
            send(kb.at[c, zz, x], xk_s.at[zz, d], xk_r.at[zz, d], xside[d])

    for d in range(2):
        send(kb.at[c, z, x], zk_s.at[d, 1], zk_r.at[d, 1], zside[d])
    kx_send(z)

    xm, xp, xo = (x + 3) % NX, (x + 1) % NX, (x + 2) % NX
    cols = (x, xm, xp, xo)
    arrived(vb.at[c, z, xm], xv_s.at[0], xv_r.at[0])
    top = vb.at[c, z, xm, pl.ds(0, 64), :]
    send(top, xv_s.at[2], xv_r.at[2], xside[0])
    vz_send(z, xm, 1, 1)
    arrived(vb.at[c, z, xp], xv_s.at[1], xv_r.at[1])
    low = vb.at[c, z, xp, pl.ds(64, 64), :]
    send(low, xv_s.at[3], xv_r.at[3], xside[1])
    vz_send(z, xp, 1, 2)
    arrived(vb.at[c, z, xo, pl.ds(0, 64), :], xv_s.at[2], xv_r.at[2])
    arrived(vb.at[c, z, xo, pl.ds(64, 64), :], xv_s.at[3], xv_r.at[3])
    vz_send(z, xo, 1, 3)
    q_copy.wait()

    row_of = i * ROWS + lax.broadcasted_iota(jnp.int32, (ROWS, 128), 0)
    lane = lax.broadcasted_iota(jnp.int32, (ROWS, 128), 1)

    def flash(za, zb):
        ck0, ck1, cvs = [], [], []
        for zz in (za, zb):
            for xx in range(NX):
                for cc in range(2):
                    first = kb[cc, zz, xx, pl.ds(192, 16), :].astype(F32)
                    second = kb[cc, zz, xx, pl.ds(208, 16), :].astype(F32)
                    ck0.append(first[:8])
                    ck1.append(first[8:])
                    cvs.append(second[:8])
        ck0 = jnp.concatenate(ck0, 0)
        ck1 = jnp.concatenate(ck1, 0)
        cvext[:, :128] = jnp.concatenate(cvs, 0).astype(BF16)
        even = jnp.concatenate([ck0, ck1], 1).astype(BF16)
        r0 = pltpu.roll(ck0, 64, 1)
        r1 = pltpu.roll(ck1, 64, 1)
        odd = jnp.concatenate(
            [jnp.where(lane < 64, r1, r0), jnp.where(lane < 64, r0, r1)], 1
        ).astype(BF16)
        zed = jnp.where(lane < 64, za, zb)
        block = (((lane // 16) % 4) * 32 + zed * 2 + (lane // 8) % 2) * 8 + lane % 8
        bias = jnp.where(block * 16 + 31 <= row_of, 0.0, LOW).astype(F32)
        extended = cvext[...]

        def pair(p, carry):
            two = q_vm[:, pl.ds(pl.multiple_of(p * 384, 128), 384)]
            for par, table in ((0, even), (1, odd)):
                h = 2 * p + par
                score = lax.dot_general(
                    two[:, 128 * par:128 * par + 256], table, (((1,), (1,)), ((), ())),
                    preferred_element_type=F32,
                ) + bias
                old = m_sc[h]
                new = jnp.maximum(old, jnp.max(score, axis=1, keepdims=True))
                weight = jnp.exp2((score - new) * COEF)
                scale = jnp.exp2((old - new) * COEF)
                m_sc[h] = new
                added = jnp.dot(weight.astype(BF16), extended, preferred_element_type=F32)
                o_sc[h] = o_sc[h] * jnp.concatenate([scale, scale], 1) + added
            return carry

        lax.fori_loop(0, PAIRS, pair, 0)

    def sources(step):
        if step == 0:
            return (z,)
        if step == 8:
            return ((z + 8) % NZ,)
        return ((z + NZ - step) % NZ, (z + step) % NZ)

    half = KROWS // 2
    for step in range(1, 12):
        if step <= 7:
            src = sources(step)
            for d in range(2):
                chunk = kb.at[c, src[d], x]
                arrived(chunk, zk_s.at[d, step], zk_r.at[d, step])
                if step < 7:
                    send(chunk, zk_s.at[d, step + 1], zk_r.at[d, step + 1], zside[d])
                else:
                    piece = kb.at[c, src[d], x, pl.ds(d * half, half), :]
                    send(piece, zk_s.at[d, 8], zk_r.at[d, 8], zside[d])
                kx_send(src[d])
            for col in range(4):
                for d in range(2):
                    arrived(vb.at[c, src[d], cols[col]], zv_s.at[d, step, col], zv_r.at[d, step, col])
                    if step < 7 or (col % 2) == d:
                        vz_send(src[d], cols[col], step + 1, col, (d,))
        if step == 8:
            far = sources(8)[0]
            for d in range(2):
                piece = kb.at[c, far, x, pl.ds(d * half, half), :]
                arrived(piece, zk_s.at[d, 8], zk_r.at[d, 8])
            kx_send(far)
            for col in range(4):
                d = col % 2
                arrived(vb.at[c, far, cols[col]], zv_s.at[d, 8, col], zv_r.at[d, 8, col])
        if 0 <= step - 1 <= 8:
            for zz in sources(step - 1):
                arrived(kb.at[c, zz, xm], xk_s.at[zz, 0], xk_r.at[zz, 0])
                arrived(kb.at[c, zz, xp], xk_s.at[zz, 1], xk_r.at[zz, 1])
                sign = 1 - 2 * (zz % 2)
                origin = (x + NX - sign) % NX
                send(
                    kb.at[c, zz, origin], xk_s.at[zz, 2], xk_r.at[zz, 2], at(x + NX + sign, z, c)
                )
        if 0 <= step - 2 <= 8:
            for zz in sources(step - 2):
                arrived(kb.at[c, zz, xo], xk_s.at[zz, 2], xk_r.at[zz, 2])
                send(kb.at[c, zz], pk_s.at[zz], pk_r.at[zz], partner)
                send(vb.at[c, zz], pv_s.at[zz], pv_r.at[zz], partner)
        if 0 <= step - 3 <= 8:
            for zz in sources(step - 3):
                arrived(kb.at[1 - c, zz], pk_s.at[zz], pk_r.at[zz])
                arrived(vb.at[1 - c, zz], pv_s.at[zz], pv_r.at[zz])
            if 1 <= step - 3 <= 7:
                flash(*sources(step - 3))
    flash(z, sources(8)[0])

    for copy in sends:
        copy.wait_send()


def select_body(q_vm, kb, vb, o_sc, picks_ref, g_ref, out_ref, s_sc, p_sc, ks, vext):
    i = lax.axis_index("ctx")
    vext[:, 128:] = jnp.ones((1024, 128), BF16)
    ks[0:64, :] = jnp.zeros((64, 1024), BF16)
    ks[256:320, :] = jnp.zeros((64, 1024), BF16)
    gate = jax.nn.sigmoid(g_ref[...])
    half_lane = lax.broadcasted_iota(jnp.int32, (DQK, 128), 1)
    small_lane = lax.broadcasted_iota(jnp.int32, (TILE, 128), 1)
    small_row = lax.broadcasted_iota(jnp.int32, (TILE, 128), 0)
    for t in range(2):
        biases = []
        for j in range(PICKS // 2):
            tiles, sides, shifts = [], [], []
            for e in range(2):
                pick = picks_ref[t, 2 * j + e]
                safe = jnp.where(pick < 0, 2 * i + t, pick)
                owner = safe // 2
                part = safe % 2
                ox, oz, oc = owner // 32, (owner // 2) % NZ, owner % 2
                tile = kb[oc, oz, ox, pl.ds(0, DQK), :].astype(F32)
                shift = part * 64 if e == 0 else (1 - part) * 64
                tiles.append(pltpu.roll(tile, shift, 1))
                start = pl.multiple_of(part * 64, 64)
                vext[128 * j + 64 * e:128 * j + 64 * e + 64, :128] = vb[oc, oz, ox, pl.ds(start, 64), :]
                sides.append(jnp.where(pick < 0, LOW, 0.0).astype(F32))
            ks[64:256, 128 * j:128 * j + 128] = jnp.where(half_lane < 64, tiles[0], tiles[1]).astype(BF16)
            bias = jnp.where(small_lane < 64, sides[0], sides[1])
            if j == 0:
                bias = jnp.where((small_lane < 64) & (small_lane > small_row), LOW, bias)
            biases.append(bias)
        for par in range(2):
            rows = jnp.concatenate(
                [
                    q_vm[64 * t:64 * t + 64, 384 * p + 128 * par:384 * p + 128 * par + 256]
                    for p in range(PAIRS)
                ],
                0,
            )
            table = ks[64 - 64 * par:320 - 64 * par, :]
            s_sc[...] = jnp.dot(rows, table, preferred_element_type=F32)
            for p in range(PAIRS):
                pieces = [
                    s_sc[64 * p:64 * p + 64, 128 * j:128 * j + 128] + biases[j]
                    for j in range(PICKS // 2)
                ]
                score = jnp.concatenate(pieces, 1)
                top_score = jnp.max(score, axis=1, keepdims=True)
                p_sc[64 * p:64 * p + 64, :] = jnp.exp2((score - top_score) * COEF).astype(BF16)
            result = jnp.dot(p_sc[...], vext[...], preferred_element_type=F32)
            for p in range(PAIRS):
                h = 2 * p + par
                rs = slice(64 * t, 64 * t + 64)
                sel = result[64 * p:64 * p + 64, :128] / result[64 * p:64 * p + 64, 128:]
                comp = o_sc[h, rs, :128] / jnp.maximum(o_sc[h, rs, 128:], 1.0)
                mixed = gate[0, rs, h:h + 1] * comp + gate[1, rs, h:h + 1] * sel
                out_ref[rs, h * DV:(h + 1) * DV] = mixed.astype(BF16)


def local(queries, keys, values, key_weights, value_weights, picks, gates):
    vmem = pl.BlockSpec(memory_space=pltpu.VMEM)
    dma = pltpu.SemaphoreType.DMA
    kb, vb, comp = pl.pallas_call(
        gather_body,
        out_shape=[
            pltpu.VMEM((2, NZ, NX, KROWS, 128), BF16),
            pltpu.VMEM((2, NZ, NX, ROWS, 128), BF16),
            pltpu.VMEM((HEADS, ROWS, 256), F32),
        ],
        in_specs=[pl.BlockSpec(memory_space=pl.ANY), vmem, vmem, vmem, vmem],
        out_specs=[vmem, vmem, vmem],
        scratch_shapes=[
            pltpu.VMEM((ROWS, HEADS * DQK), BF16),
            pltpu.VMEM((16, DQK), BF16),
            pltpu.VMEM((16, DV), BF16),
            pltpu.VMEM((HEADS, ROWS, 128), F32),
            pltpu.VMEM((128, 256), BF16),
            dma,
            dma((2,)), dma((2,)),
            dma((2, 9)), dma((2, 9)),
            dma((2, 9, 4)), dma((2, 9, 4)),
            dma((4,)), dma((4,)),
            dma((NZ, 3)), dma((NZ, 3)),
            dma((NZ,)), dma((NZ,)),
            dma((NZ,)), dma((NZ,)),
        ],
        compiler_params=pltpu.CompilerParams(
            collective_id=0, has_side_effects=True, vmem_limit_bytes=32 * 1024 * 1024
        ),
        name="gather_compressed",
    )(queries, keys, values, key_weights, value_weights)
    return pl.pallas_call(
        select_body,
        out_shape=jax.ShapeDtypeStruct((ROWS, HEADS * DV), BF16),
        in_specs=[vmem, vmem, vmem, vmem, pl.BlockSpec(memory_space=pltpu.SMEM), vmem],
        out_specs=vmem,
        scratch_shapes=[
            pltpu.VMEM((PAIRS * TILE, 1024), F32),
            pltpu.VMEM((PAIRS * TILE, 1024), BF16),
            pltpu.VMEM((320, 1024), BF16),
            pltpu.VMEM((1024, 256), BF16),
        ],
        compiler_params=pltpu.CompilerParams(vmem_limit_bytes=32 * 1024 * 1024),
        name="selected_mix",
    )(queries, kb, vb, comp, picks, gates)


def solution(mesh):
    in_specs = (
        P("ctx", "kv"), P("ctx", "kv"), P("ctx", "kv"), P(None, "kv"), P(None, "kv"),
        P("ctx", None), P(None, "ctx", "kv"),
    )
    return jax.shard_map(
        local, mesh=mesh, in_specs=in_specs, out_specs=P("ctx", "kv"), check_vma=False
    )
```

time: 488 us -> 89.5 us (0.18)
  waiting for transfers between devices: 257 us -> 0 us
  blocking collectives: 121 us -> 0 us
  Pallas kernels: 0 us -> 82.5 us
  local copies, waits for them, and re-layouts: 37.9 us -> 5.72 us
  matrix products: 26.7 us -> 0 us
  other arithmetic: 25 us -> 0 us
  starting transfers between devices: 18.8 us -> 0 us
    ppermute x1 -> x0, waiting for transfers between devices: 168 us -> none  [passed_along(): return lax.ppermute(value, axis, pairs)]
    all_to_all x2 -> x0, waiting for transfers between devices: 89.4 us -> none  [the longest x1 89.4 us: local(): lax.all_to_all(reply_values, CTX, split_axis=0, concat_axis=0, tiled=True)]
    all_gather x6 -> x0, blocking collectives: 85.3 us -> none  [all_blocks(): tiles = lax.all_gather(tiles, axes[k])]
    pallas_call x0 -> x2, Pallas kernels: none -> 82.5 us  [the longest x1 77.6 us: local(): pl.pallas_call(gather_body, out_shape=[pltpu.VMEM((2, NZ, NX, KROWS, 128)...]
    all_to_all x1 -> x0, blocking collectives: 35.2 us -> none  [local(): lax.all_to_all(wanted.reshape(shard_count, 1), CTX, split_axis=0, concat_...]
    dot_general x14 -> x0, matrix products: 26.7 us -> none  [the longest x2 8.74 us: select_one(): jnp.einsum('rhk,kd->rhd', weights.astype(jnp.bfloat16), value_set, prefer...]
    all_to_all x2 -> x0, starting transfers between devices: 15.7 us -> none  [the longest x1 9.11 us: local(): lax.all_to_all(reply_keys, CTX, split_axis=0, concat_axis=0, tiled=True)]
    convert_element_type x4 -> x0, local copies, waits for them, and re-layouts: 10.8 us -> none  [the longest x1 6.79 us: local(): reply_keys = jnp.einsum('nt,trd->nrd', onehot, own_keys, preferred_elemen...]
  transfers between devices with their start and end apart: 3 -> 0, of which waited for: 2 -> 0; matrix products, arithmetic and copies ran while one was open for 9% -> 0% of each run, Pallas kernels for 0% -> 0%
where the time goes in v1:
time: 89.5 us; the launch traced here: 88.2 us
  Pallas kernels  82.5 us (92%)
  local copies, waits for them, and re-layouts  5.72 us (6%)
    pallas_call x1, Pallas kernels, local(): pl.pallas_call(gather_body, out_shape=[pltpu.VMEM((2, NZ, NX, KROWS, 128)...  77.6 us
    unnamed x12, local copies, waits for them, and re-layouts  5.72 us
    pallas_call x1, Pallas kernels, local(): pl.pallas_call(select_body, out_shape=jax.ShapeDtypeStruct((ROWS, HEADS *...  4.92 us

profile of v1, /device:TPU:1, one launch (start us, length us, event | category | flops | bytes accessed | tf_op | source)
XLA Modules:
  0.0 88.2 jit_solution(5882630990534977276)
XLA Ops:
  0.0 0.9 %copy.8.k_ref = bf16[128,192]{1,0:T(8,128)(2,1)S(1)} copy(bf16[128,192]{0,1:T(8,128)(2,1)} %param.8) | data formatting | bytes 98304 | tf_op args[1]
  0.9 0.8 copy.9.g_ref
  1.7 0.0 copy-start
  1.7 1.1 %copy-done = bf16[128,2688]{1,0:T(8,128)(2,1)S(1)} copy-done((bf16[128,2688]{1,0:T(8,128)(2,1)S(1)}, bf16[128,2688]{1,0:T(8,128)(2,1)}, u32[]{:S(2)}) %copy-start) | copy-done | bytes 688152
  2.8 0.0 copy-start.1
  2.8 0.8 copy-done.1
  3.6 0.0 copy-start.2
  3.6 0.8 copy-done.2
  4.3 0.0 copy-start.3
  4.3 0.7 copy-done.3
  5.1 77.6 %gather_compressed.1 = (bf16[2,16,4,224,128]{4,3,2,1,0:T(8,128)(2,1)S(1)}, bf16[2,16,4,128,128]{4,3,2,1,0:T(8,128)(2,1)S(1)}, f32[14,128,256]{2,1,0:T(8,128)S(1)}) custom-call(bf16[128,2688]{1,0:T(8,128)(2,1)S(1)} %copy-done, bf16[128,192]{1,0:T(8,128)(2,1)S(1)} %copy.8.k_ref, bf16[128,128]{1,0:T(8,128)(2,1)S(1)} %copy-done.1, f32[32,192]{1,0:T(8,128)S(1)} %copy-done.2, ...), custom_call_target="tpu_custom_call" | custom-call | tf_op jit(solution)/shard_map/gather_compressed/pallas_call | solution.py:297
  82.6 0.0 copy-start.4
  82.7 0.7 copy-done.4
  83.3 4.9 %selected_mix.1 = bf16[128,1792]{1,0:T(8,128)(2,1)} custom-call(bf16[128,2688]{1,0:T(8,128)(2,1)S(1)} %copy-done, bf16[2,16,4,224,128]{4,3,2,1,0:T(8,128)(2,1)S(1)} %get-tuple-element.8.kb, bf16[2,16,4,128,128]{4,3,2,1,0:T(8,128)(2,1)S(1)} %get-tuple-element.9.vb, f32[14,128,256]{2,1,0:T(8,128)S(1)} %get-tuple-element.10.o_sc, s32[2,16]{1,0:T(2,128)S(1)} %copy-done.4, ...), custom_call_target="tpu_custom_call" | custom-call | tf_op jit(solution)/shard_map/selected_mix/pallas_call | solution.py:326
Async XLA Ops:
  1.7 1.1 %copy-start = (bf16[128,2688]{1,0:T(8,128)(2,1)S(1)}, bf16[128,2688]{1,0:T(8,128)(2,1)}, u32[]{:S(2)}) copy-start(bf16[128,2688]{1,0:T(8,128)(2,1)} %q_vm.1) | copy-start | bytes 2064388
  2.8 0.8 copy-start.1
  3.6 0.8 copy-start.2
  4.3 0.7 copy-start.3
  82.6 0.7 copy-start.4

commit v2 on v1

v2 whole, which is shorter than its diff:
```python
import jax
import jax.numpy as jnp
from jax import lax
from jax.experimental import pallas as pl
from jax.experimental.pallas import tpu as pltpu
from jax.sharding import PartitionSpec as P

NX = 4
NZ = 16
HEADS = 14
PAIRS = HEADS // 2
DQK = 192
DV = 128
ROWS = 128
TILE = 64
PICKS = 16
CROWS = 48
KROWS = 2 * DQK + CROWS
LOW = -1e30
FLOOR = -1e29
COEF = DQK ** (-0.5) * 1.4426950408889634
F32 = jnp.float32
BF16 = jnp.bfloat16
MESH = pl.DeviceIdType.MESH


def guard(cond, step):
    if isinstance(cond, bool):
        if cond:
            step()
    else:
        pl.when(cond)(step)


def gather_body(
    q_any, kt_any, v_any, kw_any, vw_any, g_any,
    kb, vb, q_vm, gate_out,
    kw, vw, g_vm, halo_src, halo_k, halo_v,
    in_s, halo_s, halo_r, ex_s, ex_r, zk_s, zk_r, zv_s, zv_r, xv_s, xv_r, xk_s, xk_r,
    pk_s, pk_r, pv_s, pv_r,
):
    i = lax.axis_index("ctx")
    x = i // 32
    z = (i // 2) % NZ
    c = i % 2

    def at(xx, zz, cc):
        return (xx % NX) * 32 + (zz % NZ) * 2 + cc

    zside = (at(x, z + 1, c), at(x, z + NZ - 1, c))
    xside = (at(x + 1, z, c), at(x + NX - 1, z, c))
    partner = at(x, z, 1 - c)
    before = (i + 127) % 128
    after = (i + 1) % 128
    xm, xp, xo = (x + 3) % NX, (x + 1) % NX, (x + 2) % NX
    cols = (x, xm, xp, xo)

    def remote(src, dst, ss, rs, target):
        return pltpu.make_async_remote_copy(
            src_ref=src, dst_ref=dst, send_sem=ss, recv_sem=rs,
            device_id={"ctx": target}, device_id_type=MESH,
        )

    def send(ref, ss, rs, target, dst=None):
        remote(ref, ref if dst is None else dst, ss, rs, target).start()

    def arrived(ref, ss, rs):
        remote(ref, ref, ss, rs, partner).wait_recv()

    def left(ref, ss, rs):
        remote(ref, ref, ss, rs, partner).wait_send()

    barrier = pltpu.get_barrier_semaphore()
    for peer in (*zside, *xside, partner, before, after):
        pl.semaphore_signal(barrier, inc=1, device_id={"ctx": peer}, device_id_type=MESH)
    own_k = kb.at[z, x, pl.ds(pl.multiple_of(c * DQK, 64), DQK), :]
    own_v = vb.at[z, x, c]
    loads = [
        pltpu.make_async_copy(src, dst, in_s.at[n])
        for n, (src, dst) in enumerate([
            (kt_any, own_k), (v_any, own_v), (kw_any, kw), (vw_any, vw), (g_any, g_vm),
            (q_any, q_vm),
        ])
    ]
    for load in loads:
        load.start()
    loads[0].wait()
    loads[1].wait()
    first = jnp.transpose(own_k[pl.ds(0, 128), :].astype(F32))
    second = jnp.transpose(own_k[pl.ds(128, 64), :].astype(F32))
    halo_src[...] = jnp.concatenate([first[:16], second[:16]], 1).astype(BF16)
    pl.semaphore_wait(barrier, 7)

    send(own_k, ex_s.at[0], ex_r.at[0], partner)
    send(own_v, ex_s.at[1], ex_r.at[1], partner)

    @pl.when(c == 0)
    def _():
        send(halo_src, halo_s.at[0], halo_r.at[0], before, halo_k)
        send(own_v.at[pl.ds(0, 16), :], halo_s.at[1], halo_r.at[1], before, halo_v)

    own_keys = [kb.at[z, col] for col in cols[1:]] + [kb.at[z, x, pl.ds(2 * DQK, CROWS), :]]
    own_values = [vb.at[z, col] for col in cols[1:]]

    def pull(step, d):
        return (z + NZ - step) % NZ if d == 0 else (z + step) % NZ

    @pl.when(c == 1)
    def _():
        spans = (pl.ds(0, DQK), pl.ds(DQK, DQK), pl.ds(2 * DQK, CROWS))
        wide = (pl.ds(0, DQK), pl.ds(DQK, DQK + CROWS))
        late = (0, 1, 1)

        def kz_send(zz, step, piece, d):
            part = kb.at[zz, x, spans[piece], :]
            send(part, zk_s.at[d, step, piece], zk_r.at[d, step, piece], zside[d])

        def kz_wait(zz, step, piece, d):
            part = kb.at[zz, x, spans[piece], :]
            arrived(part, zk_s.at[d, step, piece], zk_r.at[d, step, piece])

        def kx_send(zz, w):
            for d in range(2):
                send(kb.at[zz, x, wide[w], :], xk_s.at[zz, d, w], xk_r.at[zz, d, w], xside[d])

        def both(q, run):
            if isinstance(q, int):
                guard(q >= 0, lambda: run(pull(q, 0)))
                guard(0 < q < 8, lambda: run(pull(q, 1)))
            else:
                guard(q >= 0, lambda: run(pull(q, 0)))
                guard(q > 0, lambda: run(pull(q, 1)))

        def x_step(q, w):
            def move(zz):
                for d, col in ((0, xm), (1, xp)):
                    arrived(kb.at[zz, col, wide[w], :], xk_s.at[zz, d, w], xk_r.at[zz, d, w])
                sign = 1 - 2 * (zz % 2)
                origin = (x + NX - sign) % NX
                send(
                    kb.at[zz, origin, wide[w], :], xk_s.at[zz, 2, w], xk_r.at[zz, 2, w],
                    at(x + NX + sign, z, c),
                )

            both(q, move)

        def p_step(q):
            def landed(zz):
                for w in range(2):
                    arrived(kb.at[zz, xo, wide[w], :], xk_s.at[zz, 2, w], xk_r.at[zz, 2, w])

            def move(zz):
                landed(zz)
                send(kb.at[zz], pk_s.at[zz], pk_r.at[zz], partner)

            def move_own():
                landed(z)
                for n, part in enumerate(own_keys):
                    send(part, pk_s.at[NZ + n], pk_r.at[NZ + n], partner)

            if isinstance(q, int):
                guard(q > 0, lambda: move(pull(q, 0)))
                guard(0 < q < 8, lambda: move(pull(q, 1)))
            else:
                guard(q > 0, lambda: (move(pull(q, 0)), move(pull(q, 1)))[0])
            guard(q == 0, move_own)

        for d in range(2):
            kz_send(z, 1, 1, d)
        arrived(kb.at[z, x, spans[0], :], ex_s.at[0], ex_r.at[0])
        for d in range(2):
            kz_send(z, 1, 0, d)
        kx_send(z, 0)
        arrived(vb.at[z, x, 0], ex_s.at[1], ex_r.at[1])
        loads[2].wait()
        loads[3].wait()
        other = kb[z, x, pl.ds(0, DQK), :].astype(F32)
        natural = jnp.concatenate(
            [
                jnp.concatenate([jnp.transpose(other[:128]), jnp.transpose(other[128:])], 1),
                jnp.concatenate([first, second], 1),
            ],
            0,
        )
        chip_v = jnp.concatenate([vb[z, x, 0], vb[z, x, 1]], 0).astype(F32)
        arrived(halo_k, halo_s.at[0], halo_r.at[0])
        arrived(halo_v, halo_s.at[1], halo_r.at[1])
        inside = (i != 127).astype(F32)

        def compress(rows, extra, weights):
            joined = jnp.concatenate([rows, extra.astype(F32) * inside], 0)
            parts = [
                jnp.sum(joined[16 * b:16 * b + 32] * weights, axis=0, keepdims=True)
                for b in range(16)
            ]
            return jnp.concatenate(parts, 0)

        ck = compress(natural, halo_k[...], kw[...])
        cv = compress(chip_v, halo_v[...], vw[...])
        own = kb.at[z, x]
        own[pl.ds(2 * DQK, 16), :] = ck[:, :128].astype(BF16)
        own[pl.ds(2 * DQK + 16, 16), :] = jnp.concatenate(
            [ck[:, 128:], jnp.zeros((16, 64), F32)], 1
        ).astype(BF16)
        own[pl.ds(2 * DQK + 32, 16), :] = cv.astype(BF16)
        for d in range(2):
            kz_send(z, 1, 2, d)
        kx_send(z, 1)
        loads[5].wait()

        def z_step(s, piece, forward):
            for d in range(2):
                zz = pull(s, d)
                kz_wait(zz, s, piece, d)
                if forward or late[piece] == d:
                    kz_send(zz, s + 1, piece, d)
                if piece != 1:
                    kx_send(zz, late[piece])

        def round_of(s, forward):
            z_step(s, 0, forward)
            z_step(s, 1, forward)
            x_step(s - 1, 0)
            z_step(s, 2, forward)
            x_step(s - 2, 1)
            p_step(s - 3)

        def loop_round(s, carry):
            round_of(s, True)
            return carry

        lax.fori_loop(1, 7, loop_round, 0)
        round_of(7, False)
        far = (z + 8) % NZ
        kz_wait(far, 8, 0, 0)
        kx_send(far, 0)
        x_step(7, 0)
        x_step(6, 1)
        kz_wait(far, 8, 1, 1)
        kz_wait(far, 8, 2, 1)
        kx_send(far, 1)
        x_step(8, 0)
        p_step(5)
        x_step(7, 1)
        p_step(6)
        x_step(8, 1)
        p_step(7)
        p_step(8)
        loads[4].wait()
        columns = jnp.concatenate(
            [g_vm[h] for h in range(HEADS)] + [jnp.zeros((4, ROWS), F32)], 0
        )
        gate_out[...] = jax.nn.sigmoid(jnp.transpose(columns))

        for zz in range(NZ):
            for d in range(3):
                for w in range(2):
                    left(kb.at[zz, x, wide[w], :], xk_s.at[zz, d, w], xk_r.at[zz, d, w])
        for k in range(1, NZ):
            zz = (z + k) % NZ
            left(kb.at[zz], pk_s.at[zz], pk_r.at[zz])
        for n, part in enumerate(own_keys):
            left(part, pk_s.at[NZ + n], pk_r.at[NZ + n])
        for s in range(1, 9):
            for piece in range(3):
                for d in range(2):
                    if s < 8 or late[piece] == d:
                        part = kb.at[z, x, spans[piece], :]
                        left(part, zk_s.at[d, s, piece], zk_r.at[d, s, piece])
        for k in range(1, NZ):
            zz = (z + k) % NZ
            arrived(vb.at[zz], pv_s.at[zz], pv_r.at[zz])
        for n, part in enumerate(own_values):
            arrived(part, pv_s.at[NZ + n], pv_r.at[NZ + n])
        left(own_k, ex_s.at[0], ex_r.at[0])
        left(own_v, ex_s.at[1], ex_r.at[1])

    @pl.when(c == 0)
    def _():
        def vz_send(zz, xx, step, col, d):
            send(vb.at[zz, xx], zv_s.at[d, step, col], zv_r.at[d, step, col], zside[d])

        def vz_wait(zz, xx, step, col, d):
            arrived(vb.at[zz, xx], zv_s.at[d, step, col], zv_r.at[d, step, col])

        def p_send(zz):
            send(vb.at[zz], pv_s.at[zz], pv_r.at[zz], partner)

        def k_wait(q):
            for d in range(2):
                zz = pull(q, d)

                def hold(zz=zz):
                    arrived(kb.at[zz], pk_s.at[zz], pk_r.at[zz])

                guard(q > 0 if d == 0 or not isinstance(q, int) else 0 < q < 8, hold)

            def hold_own():
                for n, part in enumerate(own_keys):
                    arrived(part, pk_s.at[NZ + n], pk_r.at[NZ + n])

            guard(q == 0, hold_own)

        arrived(vb.at[z, x, 1], ex_s.at[1], ex_r.at[1])
        for d in range(2):
            send(vb.at[z, x], xv_s.at[d], xv_r.at[d], xside[d])
        for d in range(2):
            vz_send(z, x, 1, 0, d)
        arrived(vb.at[z, xm], xv_s.at[0], xv_r.at[0])
        send(vb.at[z, xm, 0], xv_s.at[2], xv_r.at[2], xside[0])
        for d in range(2):
            vz_send(z, xm, 1, 1, d)
        arrived(vb.at[z, xp], xv_s.at[1], xv_r.at[1])
        send(vb.at[z, xp, 1], xv_s.at[3], xv_r.at[3], xside[1])
        for d in range(2):
            vz_send(z, xp, 1, 2, d)
        arrived(vb.at[z, xo, 0], xv_s.at[2], xv_r.at[2])
        arrived(vb.at[z, xo, 1], xv_s.at[3], xv_r.at[3])
        for d in range(2):
            vz_send(z, xo, 1, 3, d)
        for n, part in enumerate(own_values):
            send(part, pv_s.at[NZ + n], pv_r.at[NZ + n], partner)
        arrived(kb.at[z, x, pl.ds(DQK, DQK), :], ex_s.at[0], ex_r.at[0])
        loads[5].wait()

        def south_wait(s):
            if isinstance(s, int):
                return
            guard(s == 4, lambda: k_wait(0))
            guard(s >= 4, lambda: k_wait(s - 3))
            guard(s == 6, lambda: k_wait(s - 2))

        def round_of(s, forward):
            for col in range(4):
                for d in range(2):
                    zz = pull(s, d)
                    vz_wait(zz, cols[col], s, col, d)
                    if forward or col % 2 == d:
                        vz_send(zz, cols[col], s + 1, col, d)
                if col == 0:
                    south_wait(s)
            for d in range(2):
                p_send(pull(s, d))

        def loop_round(s, carry):
            round_of(s, True)
            return carry

        lax.fori_loop(1, 7, loop_round, 0)
        round_of(7, False)
        far = (z + 8) % NZ
        vz_wait(far, cols[0], 8, 0, 0)
        vz_wait(far, cols[1], 8, 1, 1)
        vz_wait(far, cols[2], 8, 2, 0)
        vz_wait(far, cols[3], 8, 3, 1)
        p_send(far)
        k_wait(5)
        k_wait(6)
        k_wait(7)
        k_wait(8)
        loads[2].wait()
        loads[3].wait()
        loads[4].wait()
        columns = jnp.concatenate(
            [g_vm[h] for h in range(HEADS)] + [jnp.zeros((4, ROWS), F32)], 0
        )
        gate_out[...] = jax.nn.sigmoid(jnp.transpose(columns))

        for k in range(1, NZ):
            zz = (z + k) % NZ
            left(vb.at[zz], pv_s.at[zz], pv_r.at[zz])
        for n, part in enumerate(own_values):
            left(part, pv_s.at[NZ + n], pv_r.at[NZ + n])
        for s in range(1, 9):
            for col in range(4):
                for d in range(2):
                    if s < 8 or col % 2 == d:
                        left(vb.at[z, x], zv_s.at[d, s, col], zv_r.at[d, s, col])
        for d in range(2):
            left(vb.at[z, x], xv_s.at[d], xv_r.at[d])
            left(vb.at[z, x, 0], xv_s.at[2 + d], xv_r.at[2 + d])
        left(own_k, ex_s.at[0], ex_r.at[0])
        left(own_v, ex_s.at[1], ex_r.at[1])
        left(halo_src, halo_s.at[0], halo_r.at[0])
        left(own_v.at[pl.ds(0, 16), :], halo_s.at[1], halo_r.at[1])


def mix_body(
    q_vm, kb, vb, gate_ref, picks_ref, out_ref, s_sc, p_sc, ks, vext, even_sc, odd_sc, bias_sc, comp_sc
):
    i = lax.axis_index("ctx")

    lane128 = lax.broadcasted_iota(jnp.int32, (256, 128), 1)
    wide_lane = lax.broadcasted_iota(jnp.int32, (ROWS, 128), 1)
    row_of = i * ROWS + lax.broadcasted_iota(jnp.int32, (ROWS, 128), 0)
    for part in range(4):
        rows = slice(256 * part, 256 * part + 256)

        def table(start):
            return jnp.concatenate(
                [
                    kb[4 * part + n // NX, n % NX, pl.ds(start, 16), :] for n in range(16)
                ],
                0,
            )

        ck0, ck1 = table(2 * DQK), table(2 * DQK + 16)
        vext[rows, :128] = table(2 * DQK + 32)
        even_sc[rows, :128] = ck0
        even_sc[rows, 128:] = ck1
        r0 = pltpu.roll(ck0.astype(F32), 64, 1)
        r1 = pltpu.roll(ck1.astype(F32), 64, 1)
        odd_sc[rows, :128] = jnp.where(lane128 < 64, r1, r0).astype(BF16)
        odd_sc[rows, 128:] = jnp.where(lane128 < 64, r0, r1).astype(BF16)
        for n in range(2):
            zed = 4 * part + 2 * n + wide_lane // 64
            block = (((wide_lane // 16) % 4) * 32 + zed * 2) * 8 + wide_lane % 16
            start = 256 * part + 128 * n
            bias_sc[:, start:start + 128] = jnp.where(block * 16 + 31 <= row_of, 0.0, LOW).astype(F32)
    vext[:, 128:] = jnp.ones((1024, 128), BF16)
    for par, table in ((0, even_sc), (1, odd_sc)):
        rows = jnp.concatenate(
            [q_vm[:, 384 * p + 128 * par:384 * p + 128 * par + 256] for p in range(PAIRS)], 0
        )
        s_sc[...] = lax.dot_general(
            rows, table[...], (((1,), (1,)), ((), ())), preferred_element_type=F32
        )
        for p in range(2 * PAIRS):
            rs = slice(64 * p, 64 * p + 64)
            score = s_sc[rs, :] + bias_sc[64 * (p % 2):64 * (p % 2) + 64, :]
            top_score = jnp.maximum(jnp.max(score, axis=1, keepdims=True), FLOOR)
            p_sc[rs, :] = jnp.exp2((score - top_score) * COEF).astype(BF16)
        result = jnp.dot(p_sc[...], vext[...], preferred_element_type=F32)
        for p in range(PAIRS):
            h = 2 * p + par
            rs = slice(128 * p, 128 * p + 128)
            comp = result[rs, :128] / jnp.maximum(result[rs, 128:], 1.0)
            comp_sc[h] = gate_ref[:, 2 * h:2 * h + 1] * comp

    ks[0:64, :] = jnp.zeros((64, 1024), BF16)
    ks[256:320, :] = jnp.zeros((64, 1024), BF16)
    half_lane = lax.broadcasted_iota(jnp.int32, (DQK, 128), 1)
    small_lane = lax.broadcasted_iota(jnp.int32, (TILE, 128), 1)
    small_row = lax.broadcasted_iota(jnp.int32, (TILE, 128), 0)
    for t in range(2):
        biases = []
        for j in range(PICKS // 2):
            tiles, sides = [], []
            for e in range(2):
                pick = picks_ref[t, 2 * j + e]
                safe = jnp.where(pick < 0, 2 * i + t, pick)
                owner = safe // 2
                part = safe % 2
                ox, oz, oc = owner // 32, (owner // 2) % NZ, owner % 2
                tile = kb[oz, ox, pl.ds(pl.multiple_of(oc * DQK, 64), DQK), :].astype(F32)
                shift = part * 64 if e == 0 else (1 - part) * 64
                tiles.append(pltpu.roll(tile, shift, 1))
                start = pl.multiple_of(part * 64, 64)
                vext[128 * j + 64 * e:128 * j + 64 * e + 64, :128] = vb[oz, ox, oc, pl.ds(start, 64), :]
                sides.append(jnp.where(pick < 0, LOW, 0.0).astype(F32))
            ks[64:256, 128 * j:128 * j + 128] = jnp.where(half_lane < 64, tiles[0], tiles[1]).astype(BF16)
            bias = jnp.where(small_lane < 64, sides[0], sides[1])
            if j == 0:
                bias = jnp.where((small_lane < 64) & (small_lane > small_row), LOW, bias)
            biases.append(bias)
        for par in range(2):
            rows = jnp.concatenate(
                [
                    q_vm[64 * t:64 * t + 64, 384 * p + 128 * par:384 * p + 128 * par + 256]
                    for p in range(PAIRS)
                ],
                0,
            )
            table = ks[64 - 64 * par:320 - 64 * par, :]
            s_sc[:448, :] = jnp.dot(rows, table, preferred_element_type=F32)
            for p in range(PAIRS):
                pieces = [
                    s_sc[64 * p:64 * p + 64, 128 * j:128 * j + 128] + biases[j]
                    for j in range(PICKS // 2)
                ]
                score = jnp.concatenate(pieces, 1)
                top_score = jnp.max(score, axis=1, keepdims=True)
                p_sc[64 * p:64 * p + 64, :] = jnp.exp2((score - top_score) * COEF).astype(BF16)
            result = jnp.dot(p_sc[:448, :], vext[...], preferred_element_type=F32)
            for p in range(PAIRS):
                h = 2 * p + par
                rs = slice(64 * t, 64 * t + 64)
                sel = result[64 * p:64 * p + 64, :128] / result[64 * p:64 * p + 64, 128:]
                mixed = comp_sc[h, rs] + gate_ref[rs, 2 * h + 1:2 * h + 2] * sel
                out_ref[rs, h * DV:(h + 1) * DV] = mixed.astype(BF16)


def local(queries, keys, values, key_weights, value_weights, picks, gates):
    vmem = pl.BlockSpec(memory_space=pltpu.VMEM)
    hbm = pl.BlockSpec(memory_space=pltpu.HBM)
    dma = pltpu.SemaphoreType.DMA
    kb, vb, rows, gate = pl.pallas_call(
        gather_body,
        out_shape=[
            pltpu.VMEM((NZ, NX, KROWS, 128), BF16),
            pltpu.VMEM((NZ, NX, 2, ROWS, 128), BF16),
            pltpu.VMEM((ROWS, HEADS * DQK), BF16),
            pltpu.VMEM((ROWS, 32), F32),
        ],
        in_specs=[hbm] * 6,
        out_specs=[vmem] * 4,
        scratch_shapes=[
            pltpu.VMEM((32, DQK), F32),
            pltpu.VMEM((32, DV), F32),
            pltpu.VMEM((HEADS, 2, ROWS), F32),
            pltpu.VMEM((16, DQK), BF16),
            pltpu.VMEM((16, DQK), BF16),
            pltpu.VMEM((16, DV), BF16),
            dma((6,)),
            dma((2,)), dma((2,)),
            dma((2,)), dma((2,)),
            dma((2, 9, 3)), dma((2, 9, 3)),
            dma((2, 9, 4)), dma((2, 9, 4)),
            dma((4,)), dma((4,)),
            dma((NZ, 3, 2)), dma((NZ, 3, 2)),
            dma((NZ + 4,)), dma((NZ + 4,)),
            dma((NZ + 3,)), dma((NZ + 3,)),
        ],
        compiler_params=pltpu.CompilerParams(
            collective_id=0, has_side_effects=True, vmem_limit_bytes=50 * 1024 * 1024
        ),
        name="gather_rows",
    )(queries, keys.T, values, key_weights, value_weights, jnp.transpose(gates, (2, 0, 1)))
    return pl.pallas_call(
        mix_body,
        out_shape=jax.ShapeDtypeStruct((ROWS, HEADS * DV), BF16),
        in_specs=[vmem] * 4 + [pl.BlockSpec(memory_space=pltpu.SMEM)],
        out_specs=vmem,
        scratch_shapes=[
            pltpu.VMEM((PAIRS * ROWS, 1024), F32),
            pltpu.VMEM((PAIRS * ROWS, 1024), BF16),
            pltpu.VMEM((320, 1024), BF16),
            pltpu.VMEM((1024, 256), BF16),
            pltpu.VMEM((1024, 256), BF16),
            pltpu.VMEM((1024, 256), BF16),
            pltpu.VMEM((ROWS, 1024), F32),
            pltpu.VMEM((HEADS, ROWS, 128), F32),
        ],
        compiler_params=pltpu.CompilerParams(vmem_limit_bytes=32 * 1024 * 1024),
        name="attend_mix",
    )(rows, kb, vb, gate, picks)


def solution(mesh):
    in_specs = (
        P("ctx", "kv"), P("ctx", "kv"), P("ctx", "kv"), P(None, "kv"), P(None, "kv"),
        P("ctx", None), P(None, "ctx", "kv"),
    )
    return jax.shard_map(
        local, mesh=mesh, in_specs=in_specs, out_specs=P("ctx", "kv"), check_vma=False
    )
```

time: 89.5 us -> 65.6 us (0.73); the launches traced: 88.2 us -> 65.5 us
  Pallas kernels: 82.5 us -> 64.8 us
  local copies, waits for them, and re-layouts: 5.72 us -> 0.67 us
    pallas_call x2, Pallas kernels: 82.5 us -> 64.8 us  [the longest x1 57.2 us: local(): pl.pallas_call(gather_body, out_shape=[pltpu.VMEM((NZ, NX, KROWS, 128), B...]
    unnamed x12 -> x2, local copies, waits for them, and re-layouts: 5.72 us -> 0.67 us
where the time goes in v2:
time: 65.6 us; the launch traced here: 65.5 us
  Pallas kernels  64.8 us (99%)
  local copies, waits for them, and re-layouts  0.67 us (1%)
    pallas_call x1, Pallas kernels, local(): pl.pallas_call(gather_body, out_shape=[pltpu.VMEM((NZ, NX, KROWS, 128), B...  57.2 us
    pallas_call x1, Pallas kernels, local(): pl.pallas_call(mix_body, out_shape=jax.ShapeDtypeStruct((ROWS, HEADS * DV...  7.61 us

profile of v2, /device:TPU:1, one launch (start us, length us, event | category | flops | bytes accessed | tf_op | source)
XLA Modules:
  0.0 65.5 jit_solution(4404320969582821814)
XLA Ops:
  0.0 57.2 %gather_rows.1 = (bf16[16,4,432,128]{3,2,1,0:T(8,128)(2,1)S(1)}, bf16[16,4,2,128,128]{4,3,2,1,0:T(8,128)(2,1)S(1)}, bf16[128,2688]{1,0:T(8,128)(2,1)S(1)}, f32[128,32]{1,0:T(8,128)S(1)}) custom-call(bf16[128,2688]{1,0:T(8,128)(2,1)} %q_any.1, bf16[192,128]{1,0:T(8,128)(2,1)} %bitcast.2, bf16[128,128]{1,0:T(8,128)(2,1)} %v_any.1, f32[32,192]{1,0:T(8,128)} %kw_any.1, ...), custom_call_target="tpu_custom_call" | custom-call | tf_op jit(solution)/shard_map/gather_rows/pallas_call | solution.py:497
  57.2 0.0 copy-start
  57.2 0.7 %copy-done = s32[2,16]{1,0:T(2,128)S(1)} copy-done((s32[2,16]{1,0:T(2,128)S(1)}, s32[2,16]{1,0:T(2,128)}, u32[]{:S(2)}) %copy-start) | copy-done | bytes 152
  57.9 7.6 %attend_mix.1 = bf16[128,1792]{1,0:T(8,128)(2,1)} custom-call(bf16[128,2688]{1,0:T(8,128)(2,1)S(1)} %get-tuple-element.9.q_vm, bf16[16,4,432,128]{3,2,1,0:T(8,128)(2,1)S(1)} %get-tuple-element.10.kb, bf16[16,4,2,128,128]{4,3,2,1,0:T(8,128)(2,1)S(1)} %get-tuple-element.11.vb, f32[128,32]{1,0:T(8,128)S(1)} %get-tuple-element.12.gate_ref, s32[2,16]{1,0:T(2,128)S(1)} %copy-done), custom_call_target="tpu_custom_call" | custom-call | tf_op jit(solution)/shard_map/attend_mix/pallas_call | solution.py:529
Async XLA Ops:
  57.2 0.7 %copy-start = (s32[2,16]{1,0:T(2,128)S(1)}, s32[2,16]{1,0:T(2,128)}, u32[]{:S(2)}) copy-start(s32[2,16]{1,0:T(2,128)} %picks_ref.1) | copy-start | bytes 388

commit v3 on v2

v3 whole, which is shorter than its diff:
```python
import jax
import jax.numpy as jnp
from jax import lax
from jax.experimental import pallas as pl
from jax.experimental.pallas import tpu as pltpu
from jax.sharding import PartitionSpec as P

NX = 4
NZ = 16
HEADS = 14
PAIRS = HEADS // 2
DQK = 192
DV = 128
ROWS = 128
TILE = 64
PICKS = 16
CROWS = 48
KROWS = 2 * DQK + CROWS
LOW = -1e30
FLOOR = -1e29
COEF = DQK ** (-0.5) * 1.4426950408889634
F32 = jnp.float32
BF16 = jnp.bfloat16
MESH = pl.DeviceIdType.MESH


def guard(cond, step):
    if isinstance(cond, bool):
        if cond:
            step()
    else:
        pl.when(cond)(step)


def gather_body(
    q_any, kt_any, v_any, kw_any, vw_any, g_any, picks_any,
    kb, vb, q_vm, gate_out, picks_out,
    kw, vw, g_vm, halo_src, halo_k, halo_v,
    in_s, halo_s, halo_r, ex_s, ex_r, zk_s, zk_r, zv_s, zv_r, xv_s, xv_r, xk_s, xk_r,
    pk_s, pk_r, pv_s, pv_r,
):
    i = lax.axis_index("ctx")
    x = i // 32
    z = (i // 2) % NZ
    c = i % 2

    def at(xx, zz, cc):
        return (xx % NX) * 32 + (zz % NZ) * 2 + cc

    zside = (at(x, z + 1, c), at(x, z + NZ - 1, c))
    xside = (at(x + 1, z, c), at(x + NX - 1, z, c))
    partner = at(x, z, 1 - c)
    before = (i + 127) % 128
    after = (i + 1) % 128
    xm, xp, xo = (x + 3) % NX, (x + 1) % NX, (x + 2) % NX
    cols = (x, xm, xp, xo)

    def remote(src, dst, ss, rs, target):
        return pltpu.make_async_remote_copy(
            src_ref=src, dst_ref=dst, send_sem=ss, recv_sem=rs,
            device_id={"ctx": target}, device_id_type=MESH,
        )

    def send(ref, ss, rs, target, dst=None):
        remote(ref, ref if dst is None else dst, ss, rs, target).start()

    def arrived(ref, ss, rs):
        remote(ref, ref, ss, rs, partner).wait_recv()

    def left(ref, ss, rs):
        remote(ref, ref, ss, rs, partner).wait_send()

    barrier = pltpu.get_barrier_semaphore()
    across = at(x + 2, z, c)
    for peer in (*zside, *xside, across, partner, before, after):
        pl.semaphore_signal(barrier, inc=1, device_id={"ctx": peer}, device_id_type=MESH)
    own_k = kb.at[z, x, pl.ds(pl.multiple_of(c * DQK, 64), DQK), :]
    own_v = vb.at[z, x, c]
    loads = [
        pltpu.make_async_copy(src, dst, in_s.at[n])
        for n, (src, dst) in enumerate([
            (kt_any, own_k), (v_any, own_v), (kw_any, kw), (vw_any, vw), (g_any, g_vm),
            (q_any, q_vm), (picks_any, picks_out),
        ])
    ]
    for load in loads:
        load.start()
    loads[0].wait()
    loads[1].wait()
    pl.semaphore_wait(barrier, 8)

    send(own_k, ex_s.at[0], ex_r.at[0], partner)
    send(own_v, ex_s.at[1], ex_r.at[1], partner)
    first_rows = own_v.at[pl.ds(0, 16), :]

    def natural_of(ref):
        return jnp.concatenate(
            [
                jnp.transpose(ref[pl.ds(0, 128), :].astype(F32)),
                jnp.transpose(ref[pl.ds(128, 64), :].astype(F32)),
            ],
            1,
        )

    def make_gate():
        loads[4].wait()
        stacked = jnp.concatenate(
            [g_vm[h] for h in range(HEADS)] + [jnp.zeros((4, ROWS), F32)], 0
        )
        gate_out[...] = jax.nn.sigmoid(jnp.transpose(stacked))

    own_keys = [kb.at[z, col] for col in cols[1:]] + [kb.at[z, x, pl.ds(2 * DQK, CROWS), :]]
    own_values = [vb.at[z, col] for col in cols[1:]]

    def pull(step, d):
        return (z + NZ - step) % NZ if d == 0 else (z + step) % NZ

    @pl.when(c == 1)
    def _():
        spans = (pl.ds(0, DQK), pl.ds(DQK, DQK), pl.ds(2 * DQK, CROWS))
        wide = (pl.ds(0, 2 * DQK), pl.ds(2 * DQK, CROWS))
        late = (0, 1, 1)

        def kz_send(zz, step, piece, d):
            part = kb.at[zz, x, spans[piece], :]
            send(part, zk_s.at[d, step, piece], zk_r.at[d, step, piece], zside[d])

        def kz_wait(zz, step, piece, d):
            part = kb.at[zz, x, spans[piece], :]
            arrived(part, zk_s.at[d, step, piece], zk_r.at[d, step, piece])

        def kx_send(zz, w):
            for d in range(2):
                send(kb.at[zz, x, wide[w], :], xk_s.at[zz, d, w], xk_r.at[zz, d, w], xside[d])

        def both(q, run):
            if isinstance(q, int):
                guard(q >= 0, lambda: run(pull(q, 0)))
                guard(0 < q < 8, lambda: run(pull(q, 1)))
            else:
                guard(q >= 0, lambda: run(pull(q, 0)))
                guard(q > 0, lambda: run(pull(q, 1)))

        def x_step(q, w):
            def move(zz):
                for d, col in ((0, xm), (1, xp)):
                    arrived(kb.at[zz, col, wide[w], :], xk_s.at[zz, d, w], xk_r.at[zz, d, w])
                sign = 1 - 2 * (zz % 2)
                origin = (x + NX - sign) % NX
                send(
                    kb.at[zz, origin, wide[w], :], xk_s.at[zz, 2, w], xk_r.at[zz, 2, w],
                    at(x + NX + sign, z, c),
                )

            both(q, move)

        def p_step(q):
            def landed(zz):
                for w in range(2):
                    arrived(kb.at[zz, xo, wide[w], :], xk_s.at[zz, 2, w], xk_r.at[zz, 2, w])

            def move(zz):
                landed(zz)
                send(kb.at[zz], pk_s.at[zz], pk_r.at[zz], partner)

            def move_own():
                landed(z)
                for n, part in enumerate(own_keys):
                    send(part, pk_s.at[NZ + n], pk_r.at[NZ + n], partner)

            if isinstance(q, int):
                guard(q > 0, lambda: move(pull(q, 0)))
                guard(0 < q < 8, lambda: move(pull(q, 1)))
            else:
                guard(q > 0, lambda: (move(pull(q, 0)), move(pull(q, 1)))[0])
            guard(q == 0, move_own)

        for d in range(2):
            kz_send(z, 1, 1, d)
        mine = natural_of(own_k)
        arrived(kb.at[z, x, spans[0], :], ex_s.at[0], ex_r.at[0])
        for d in range(2):
            kz_send(z, 1, 0, d)
        kx_send(z, 0)
        arrived(vb.at[z, x, 0], ex_s.at[1], ex_r.at[1])
        loads[2].wait()
        loads[3].wait()
        natural = jnp.concatenate([natural_of(kb.at[z, x, spans[0], :]), mine], 0)
        chip_v = jnp.concatenate([vb[z, x, 0], vb[z, x, 1]], 0).astype(F32)
        arrived(halo_k, halo_s.at[0], halo_r.at[0])
        arrived(halo_v, halo_s.at[1], halo_r.at[1])
        inside = (i != 127).astype(F32)

        def compress(rows, extra, weights):
            joined = jnp.concatenate([rows, extra.astype(F32) * inside], 0)
            parts = [
                jnp.sum(joined[16 * b:16 * b + 32] * weights, axis=0, keepdims=True)
                for b in range(16)
            ]
            return jnp.concatenate(parts, 0)

        ck = compress(natural, halo_k[...], kw[...])
        cv = compress(chip_v, halo_v[...], vw[...])
        own = kb.at[z, x]
        own[pl.ds(2 * DQK, 16), :] = ck[:, :128].astype(BF16)
        own[pl.ds(2 * DQK + 16, 16), :] = jnp.concatenate(
            [ck[:, 128:], jnp.zeros((16, 64), F32)], 1
        ).astype(BF16)
        own[pl.ds(2 * DQK + 32, 16), :] = cv.astype(BF16)
        for d in range(2):
            kz_send(z, 1, 2, d)
        kx_send(z, 1)
        left(own_k, ex_s.at[0], ex_r.at[0])
        left(own_v, ex_s.at[1], ex_r.at[1])

        def kz_left(step, pieces=(0, 1, 2)):
            for piece in pieces:
                for d in range(2):
                    if not isinstance(step, int) or step < 8 or late[piece] == d:
                        part = kb.at[z, x, spans[piece], :]
                        left(part, zk_s.at[d, step, piece], zk_r.at[d, step, piece])

        def kx_left(q, w):
            def run(zz):
                for d in range(3):
                    left(kb.at[zz, x, wide[w], :], xk_s.at[zz, d, w], xk_r.at[zz, d, w])

            both(q, run)

        def pk_left(q):
            def run(zz):
                left(kb.at[zz], pk_s.at[zz], pk_r.at[zz])

            def run_own():
                for n, part in enumerate(own_keys):
                    left(part, pk_s.at[NZ + n], pk_r.at[NZ + n])

            if isinstance(q, int):
                guard(q > 0, lambda: run(pull(q, 0)))
                guard(0 < q < 8, lambda: run(pull(q, 1)))
            else:
                guard(q > 0, lambda: (run(pull(q, 0)), run(pull(q, 1)))[0])
            guard(q == 0, run_own)

        def z_step(s, piece, forward):
            for d in range(2):
                zz = pull(s, d)
                kz_wait(zz, s, piece, d)
                if forward or late[piece] == d:
                    kz_send(zz, s + 1, piece, d)
                if piece != 1:
                    kx_send(zz, piece // 2)

        def round_of(s, forward):
            z_step(s, 1, forward)
            z_step(s, 0, forward)
            z_step(s, 2, forward)
            x_step(s - 1, 0)
            x_step(s - 2, 1)
            p_step(s - 3)
            guard(s >= 2, lambda: kz_left(s - 1))
            kx_left(s - 2, 0)
            kx_left(s - 3, 1)
            pk_left(s - 4)

        def loop_round(s, carry):
            round_of(s, True)
            return carry

        lax.fori_loop(1, 7, loop_round, 0)
        round_of(7, False)
        far = (z + 8) % NZ
        kz_wait(far, 8, 1, 1)
        kz_wait(far, 8, 0, 0)
        kx_send(far, 0)
        kz_wait(far, 8, 2, 1)
        kx_send(far, 1)
        make_gate()
        loads[5].wait()
        loads[6].wait()
        for s in range(8, 9 + 3):
            if s - 1 <= 8:
                x_step(s - 1, 0)
            if s - 2 <= 8:
                x_step(s - 2, 1)
            if s - 3 <= 8:
                p_step(s - 3)
        kz_left(7)
        kz_left(8)
        for q in range(max(0, 6), 9):
            kx_left(q, 0)
        for q in range(max(0, 5), 9):
            kx_left(q, 1)
        for q in range(max(0, 4), 9):
            pk_left(q)
        for k in range(1, NZ):
            zz = (z + k) % NZ
            arrived(vb.at[zz], pv_s.at[zz], pv_r.at[zz])
        for n, part in enumerate(own_values):
            arrived(part, pv_s.at[NZ + n], pv_r.at[NZ + n])

    @pl.when(c == 0)
    def _():
        def vz_send(zz, xx, step, col, d):
            send(vb.at[zz, xx], zv_s.at[d, step, col], zv_r.at[d, step, col], zside[d])

        def vz_wait(zz, xx, step, col, d):
            arrived(vb.at[zz, xx], zv_s.at[d, step, col], zv_r.at[d, step, col])

        def p_send(zz):
            send(vb.at[zz], pv_s.at[zz], pv_r.at[zz], partner)

        def k_wait(q):
            for d in range(2):
                zz = pull(q, d)

                def hold(zz=zz):
                    arrived(kb.at[zz], pk_s.at[zz], pk_r.at[zz])

                guard(q > 0 if d == 0 or not isinstance(q, int) else 0 < q < 8, hold)

            def hold_own():
                for n, part in enumerate(own_keys):
                    arrived(part, pk_s.at[NZ + n], pk_r.at[NZ + n])

            guard(q == 0, hold_own)

        send(first_rows, halo_s.at[1], halo_r.at[1], before, halo_v)
        halo_src[...] = natural_of(own_k)[:16].astype(BF16)
        arrived(vb.at[z, x, 1], ex_s.at[1], ex_r.at[1])
        for d in range(2):
            send(vb.at[z, x], xv_s.at[d], xv_r.at[d], xside[d])
        send(vb.at[z, x], xv_s.at[2], xv_r.at[2], across)
        for d in range(2):
            vz_send(z, x, 1, 0, d)
        send(halo_src, halo_s.at[0], halo_r.at[0], before, halo_k)
        arrived(vb.at[z, xm], xv_s.at[0], xv_r.at[0])
        for d in range(2):
            vz_send(z, xm, 1, 1, d)
        arrived(vb.at[z, xp], xv_s.at[1], xv_r.at[1])
        for d in range(2):
            vz_send(z, xp, 1, 2, d)
        arrived(vb.at[z, xo], xv_s.at[2], xv_r.at[2])
        for d in range(2):
            vz_send(z, xo, 1, 3, d)
        for n, part in enumerate(own_values):
            send(part, pv_s.at[NZ + n], pv_r.at[NZ + n], partner)
        arrived(kb.at[z, x, pl.ds(DQK, DQK), :], ex_s.at[0], ex_r.at[0])
        for d in range(3):
            left(vb.at[z, x], xv_s.at[d], xv_r.at[d])
        left(own_k, ex_s.at[0], ex_r.at[0])
        left(own_v, ex_s.at[1], ex_r.at[1])
        left(halo_src, halo_s.at[0], halo_r.at[0])
        left(first_rows, halo_s.at[1], halo_r.at[1])

        def vz_left(step):
            for col in range(4):
                for d in range(2):
                    if not isinstance(step, int) or step < 8 or col % 2 == d:
                        left(vb.at[z, x], zv_s.at[d, step, col], zv_r.at[d, step, col])

        def pv_left(step):
            zz = pull(step, 0)
            left(vb.at[zz], pv_s.at[zz], pv_r.at[zz])
            if not isinstance(step, int) or step != 8:
                zz = pull(step, 1)
                left(vb.at[zz], pv_s.at[zz], pv_r.at[zz])

        def round_of(s, forward):
            for col in range(4):
                for d in range(2):
                    zz = pull(s, d)
                    vz_wait(zz, cols[col], s, col, d)
                    if forward or col % 2 == d:
                        vz_send(zz, cols[col], s + 1, col, d)
            for d in range(2):
                p_send(pull(s, d))
            guard(s >= 2, lambda: vz_left(s - 1))
            guard(s >= 3, lambda: pv_left(s - 2))

        def loop_round(s, carry):
            round_of(s, True)
            return carry

        lax.fori_loop(1, 7, loop_round, 0)
        round_of(7, False)
        far = (z + 8) % NZ
        make_gate()
        for load in (loads[2], loads[3], loads[5], loads[6]):
            load.wait()
        vz_wait(far, cols[0], 8, 0, 0)
        vz_wait(far, cols[1], 8, 1, 1)
        vz_wait(far, cols[2], 8, 2, 0)
        vz_wait(far, cols[3], 8, 3, 1)
        p_send(far)
        for n, part in enumerate(own_values):
            left(part, pv_s.at[NZ + n], pv_r.at[NZ + n])
        for step in range(6, 9):
            pv_left(step)
        vz_left(7)
        vz_left(8)
        for q in range(9):
            k_wait(q)


def mix_body(
    q_vm, kb, vb, gate_ref, picks_ref, out_ref, s_sc, p_sc, ks, vext, even_sc, odd_sc, bias_sc, comp_sc
):
    i = lax.axis_index("ctx")
    for n in range(3):
        vext[n, :, 128:] = jnp.ones((1024, 128), BF16)
    for n in range(2):
        ks[n, 0:64, :] = jnp.zeros((64, 1024), BF16)
        ks[n, 256:320, :] = jnp.zeros((64, 1024), BF16)

    lane128 = lax.broadcasted_iota(jnp.int32, (256, 128), 1)
    wide_lane = lax.broadcasted_iota(jnp.int32, (ROWS, 128), 1)
    row_of = i * ROWS + lax.broadcasted_iota(jnp.int32, (ROWS, 128), 0)
    for part in range(4):
        rows = slice(256 * part, 256 * part + 256)

        def table(start):
            return jnp.concatenate(
                [
                    kb[4 * part + n // NX, n % NX, pl.ds(start, 16), :] for n in range(16)
                ],
                0,
            )

        ck0, ck1 = table(2 * DQK), table(2 * DQK + 16)
        vext[2, rows, :128] = table(2 * DQK + 32)
        even_sc[rows, :128] = ck0
        even_sc[rows, 128:] = ck1
        r0 = pltpu.roll(ck0.astype(F32), 64, 1)
        r1 = pltpu.roll(ck1.astype(F32), 64, 1)
        odd_sc[rows, :128] = jnp.where(lane128 < 64, r1, r0).astype(BF16)
        odd_sc[rows, 128:] = jnp.where(lane128 < 64, r0, r1).astype(BF16)
        for n in range(2):
            zed = 4 * part + 2 * n + wide_lane // 64
            block = (((wide_lane // 16) % 4) * 32 + zed * 2) * 8 + wide_lane % 16
            start = 256 * part + 128 * n
            bias_sc[:, start:start + 128] = jnp.where(block * 16 + 31 <= row_of, 0.0, LOW).astype(F32)

    half_lane = lax.broadcasted_iota(jnp.int32, (DQK, 128), 1)
    small_lane = lax.broadcasted_iota(jnp.int32, (TILE, 128), 1)
    small_row = lax.broadcasted_iota(jnp.int32, (TILE, 128), 0)
    biases = {0: [], 1: []}

    def pick_tables(t):
        for j in range(PICKS // 2):
            tiles, sides = [], []
            for e in range(2):
                pick = picks_ref[t, 2 * j + e]
                safe = jnp.where(pick < 0, 2 * i + t, pick)
                owner = safe // 2
                part = safe % 2
                ox, oz, oc = owner // 32, (owner // 2) % NZ, owner % 2
                tile = kb[oz, ox, pl.ds(pl.multiple_of(oc * DQK, 64), DQK), :].astype(F32)
                shift = part * 64 if e == 0 else (1 - part) * 64
                tiles.append(pltpu.roll(tile, shift, 1))
                start = pl.multiple_of(part * 64, 64)
                at = 128 * j + 64 * e
                vext[t, at:at + 64, :128] = vb[oz, ox, oc, pl.ds(start, 64), :]
                sides.append(jnp.where(pick < 0, LOW, 0.0).astype(F32))
            ks[t, 64:256, 128 * j:128 * j + 128] = jnp.where(
                half_lane < 64, tiles[0], tiles[1]
            ).astype(BF16)
            bias = jnp.where(small_lane < 64, sides[0], sides[1])
            if j == 0:
                bias = jnp.where((small_lane < 64) & (small_lane > small_row), LOW, bias)
            biases[t].append(bias)

    def queries_of(start, count, par):
        return jnp.concatenate(
            [
                q_vm[start:start + count, 384 * p + 128 * par:384 * p + 128 * par + 256]
                for p in range(PAIRS)
            ],
            0,
        )

    def scores(stage, buf):
        kind, par = stage
        if kind == 2:
            table = (even_sc, odd_sc)[par]
            s_sc[buf] = lax.dot_general(
                queries_of(0, ROWS, par), table[...], (((1,), (1,)), ((), ())),
                preferred_element_type=F32,
            )
        else:
            table = ks[kind, 64 - 64 * par:320 - 64 * par, :]
            s_sc[buf, :448, :] = jnp.dot(
                queries_of(64 * kind, 64, par), table, preferred_element_type=F32
            )

    def finish(stage, buf):
        kind, par = stage
        count = 2 * PAIRS if kind == 2 else PAIRS
        for p in range(count):
            rs = slice(64 * p, 64 * p + 64)
            if kind == 2:
                score = s_sc[buf, rs, :] + bias_sc[64 * (p % 2):64 * (p % 2) + 64, :]
            else:
                score = jnp.concatenate(
                    [
                        s_sc[buf, rs, 128 * j:128 * j + 128] + biases[kind][j]
                        for j in range(PICKS // 2)
                    ],
                    1,
                )
            top_score = jnp.maximum(jnp.max(score, axis=1, keepdims=True), FLOOR)
            p_sc[buf, rs, :] = jnp.exp2((score - top_score) * COEF).astype(BF16)
        result = jnp.dot(p_sc[buf, :64 * count, :], vext[kind], preferred_element_type=F32)
        for p in range(PAIRS):
            h = 2 * p + par
            if kind == 2:
                rs = slice(128 * p, 128 * p + 128)
                comp = result[rs, :128] / jnp.maximum(result[rs, 128:], 1.0)
                comp_sc[h] = gate_ref[:, 2 * h:2 * h + 1] * comp
            else:
                rs = slice(64 * kind, 64 * kind + 64)
                sel = result[64 * p:64 * p + 64, :128] / result[64 * p:64 * p + 64, 128:]
                mixed = comp_sc[h, rs] + gate_ref[rs, 2 * h + 1:2 * h + 2] * sel
                out_ref[rs, h * DV:(h + 1) * DV] = mixed.astype(BF16)

    stages = [(2, 0), (2, 1), (0, 0), (0, 1), (1, 0), (1, 1)]
    for n, stage in enumerate(stages):
        if n == 0:
            scores(stage, 0)
            pick_tables(0)
        if n + 1 < len(stages):
            scores(stages[n + 1], (n + 1) % 2)
        if n == 1:
            pick_tables(1)
        finish(stage, n % 2)


def local(queries, keys, values, key_weights, value_weights, picks, gates):
    vmem = pl.BlockSpec(memory_space=pltpu.VMEM)
    hbm = pl.BlockSpec(memory_space=pltpu.HBM)
    dma = pltpu.SemaphoreType.DMA
    kb, vb, rows, gate, listed = pl.pallas_call(
        gather_body,
        out_shape=[
            pltpu.VMEM((NZ, NX, KROWS, 128), BF16),
            pltpu.VMEM((NZ, NX, 2, ROWS, 128), BF16),
            pltpu.VMEM((ROWS, HEADS * DQK), BF16),
            pltpu.VMEM((ROWS, 32), F32),
            pltpu.SMEM((2, PICKS), jnp.int32),
        ],
        in_specs=[hbm] * 7,
        out_specs=[vmem] * 4 + [pl.BlockSpec(memory_space=pltpu.SMEM)],
        scratch_shapes=[
            pltpu.VMEM((32, DQK), F32),
            pltpu.VMEM((32, DV), F32),
            pltpu.VMEM((HEADS, 2, ROWS), F32),
            pltpu.VMEM((16, DQK), BF16),
            pltpu.VMEM((16, DQK), BF16),
            pltpu.VMEM((16, DV), BF16),
            dma((7,)),
            dma((2,)), dma((2,)),
            dma((2,)), dma((2,)),
            dma((2, 9, 3)), dma((2, 9, 3)),
            dma((2, 9, 4)), dma((2, 9, 4)),
            dma((3,)), dma((3,)),
            dma((NZ, 3, 2)), dma((NZ, 3, 2)),
            dma((NZ + 4,)), dma((NZ + 4,)),
            dma((NZ + 3,)), dma((NZ + 3,)),
        ],
        compiler_params=pltpu.CompilerParams(
            collective_id=0, has_side_effects=True, vmem_limit_bytes=50 * 1024 * 1024
        ),
        name="gather_rows",
    )(queries, keys.T, values, key_weights, value_weights, jnp.transpose(gates, (2, 0, 1)), picks)
    return pl.pallas_call(
        mix_body,
        out_shape=jax.ShapeDtypeStruct((ROWS, HEADS * DV), BF16),
        in_specs=[vmem] * 4 + [pl.BlockSpec(memory_space=pltpu.SMEM)],
        out_specs=vmem,
        scratch_shapes=[
            pltpu.VMEM((2, PAIRS * ROWS, 1024), F32),
            pltpu.VMEM((2, PAIRS * ROWS, 1024), BF16),
            pltpu.VMEM((2, 320, 1024), BF16),
            pltpu.VMEM((3, 1024, 256), BF16),
            pltpu.VMEM((1024, 256), BF16),
            pltpu.VMEM((1024, 256), BF16),
            pltpu.VMEM((ROWS, 1024), F32),
            pltpu.VMEM((HEADS, ROWS, 128), F32),
        ],
        compiler_params=pltpu.CompilerParams(vmem_limit_bytes=32 * 1024 * 1024),
        name="attend_mix",
    )(rows, kb, vb, gate, listed)


def solution(mesh):
    in_specs = (
        P("ctx", "kv"), P("ctx", "kv"), P("ctx", "kv"), P(None, "kv"), P(None, "kv"),
        P("ctx", None), P(None, "ctx", "kv"),
    )
    return jax.shard_map(
        local, mesh=mesh, in_specs=in_specs, out_specs=P("ctx", "kv"), check_vma=False
    )
```

time: 65.6 us -> 64.2 us (0.979)
  Pallas kernels: 64.8 us -> 64.1 us
  local copies, waits for them, and re-layouts: 0.67 us -> 0 us
    pallas_call x1, Pallas kernels: 7.61 us -> 6.73 us  [local(): pl.pallas_call(mix_body, out_shape=jax.ShapeDtypeStruct((ROWS, HEADS * DV...]
    unnamed x2 -> x0, local copies, waits for them, and re-layouts: 0.67 us -> none
where the time goes in v3:
time: 64.2 us; the launch traced here: 64.1 us
  Pallas kernels  64.1 us (100%)
    pallas_call x1, Pallas kernels, local(): pl.pallas_call(gather_body, out_shape=[pltpu.VMEM((NZ, NX, KROWS, 128), B...  57.3 us
    pallas_call x1, Pallas kernels, local(): pl.pallas_call(mix_body, out_shape=jax.ShapeDtypeStruct((ROWS, HEADS * DV...  6.73 us

profile of v3, /device:TPU:1, one launch (start us, length us, event | category | flops | bytes accessed | tf_op | source)
XLA Modules:
  0.0 64.1 jit_solution(2585893486989120875)
XLA Ops:
  0.0 57.3 %gather_rows.1 = (bf16[16,4,432,128]{3,2,1,0:T(8,128)(2,1)S(1)}, bf16[16,4,2,128,128]{4,3,2,1,0:T(8,128)(2,1)S(1)}, bf16[128,2688]{1,0:T(8,128)(2,1)S(1)}, f32[128,32]{1,0:T(8,128)S(1)}, s32[2,16]{1,0:T(2,128)S(4)}) custom-call(bf16[128,2688]{1,0:T(8,128)(2,1)} %q_any.1, bf16[192,128]{1,0:T(8,128)(2,1)} %bitcast.2, bf16[128,128]{1,0:T(8,128)(2,1)} %v_any.1, ...), custom_call_target="tpu_custom_call" | custom-call | tf_op jit(solution)/shard_map/gather_rows/pallas_call | solution.py:542
  57.3 6.7 %attend_mix.1 = bf16[128,1792]{1,0:T(8,128)(2,1)} custom-call(bf16[128,2688]{1,0:T(8,128)(2,1)S(1)} %get-tuple-element.10.q_vm, bf16[16,4,432,128]{3,2,1,0:T(8,128)(2,1)S(1)} %get-tuple-element.11.kb, bf16[16,4,2,128,128]{4,3,2,1,0:T(8,128)(2,1)S(1)} %get-tuple-element.12.vb, f32[128,32]{1,0:T(8,128)S(1)} %get-tuple-element.13.gate_ref, ...), custom_call_target="tpu_custom_call" | custom-call | tf_op jit(solution)/shard_map/attend_mix/pallas_call | solution.py:575

commit v4 on v3

--- a/solution.py
+++ b/solution.py
@@ -111,6 +111,9 @@
 
     own_keys = [kb.at[z, col] for col in cols[1:]] + [kb.at[z, x, pl.ds(2 * DQK, CROWS), :]]
     own_values = [vb.at[z, col] for col in cols[1:]]
+    last = (z + 8) % NZ
+    last_keys = [kb.at[last, col] for col in cols]
+    last_values = [vb.at[last, col] for col in cols]
 
     def pull(step, d):
         return (z + NZ - step) % NZ if d == 0 else (z + step) % NZ
@@ -169,8 +172,13 @@
                     send(part, pk_s.at[NZ + n], pk_r.at[NZ + n], partner)
 
             if isinstance(q, int):
-                guard(q > 0, lambda: move(pull(q, 0)))
+                guard(0 < q < 8, lambda: move(pull(q, 0)))
                 guard(0 < q < 8, lambda: move(pull(q, 1)))
+                if q == 8:
+                    for n in range(3):
+                        send(last_keys[n], pk_s.at[NZ + 4 + n], pk_r.at[NZ + 4 + n], partner)
+                    landed(last)
+                    send(last_keys[3], pk_s.at[NZ + 7], pk_r.at[NZ + 7], partner)
             else:
                 guard(q > 0, lambda: (move(pull(q, 0)), move(pull(q, 1)))[0])
             guard(q == 0, move_own)
@@ -236,8 +244,11 @@
                     left(part, pk_s.at[NZ + n], pk_r.at[NZ + n])
 
             if isinstance(q, int):
-                guard(q > 0, lambda: run(pull(q, 0)))
+                guard(0 < q < 8, lambda: run(pull(q, 0)))
                 guard(0 < q < 8, lambda: run(pull(q, 1)))
+                if q == 8:
+                    for n, part in enumerate(last_keys):
+                        left(part, pk_s.at[NZ + 4 + n], pk_r.at[NZ + 4 + n])
             else:
                 guard(q > 0, lambda: (run(pull(q, 0)), run(pull(q, 1)))[0])
             guard(q == 0, run_own)
@@ -294,8 +305,11 @@
         for q in range(max(0, 4), 9):
             pk_left(q)
         for k in range(1, NZ):
-            zz = (z + k) % NZ
-            arrived(vb.at[zz], pv_s.at[zz], pv_r.at[zz])
+            if k != 8:
+                zz = (z + k) % NZ
+                arrived(vb.at[zz], pv_s.at[zz], pv_r.at[zz])
+        for n, part in enumerate(last_values):
+            arrived(part, pv_s.at[NZ + 3 + n], pv_r.at[NZ + 3 + n])
         for n, part in enumerate(own_values):
             arrived(part, pv_s.at[NZ + n], pv_r.at[NZ + n])
 
@@ -311,13 +325,13 @@
             send(vb.at[zz], pv_s.at[zz], pv_r.at[zz], partner)
 
         def k_wait(q):
-            for d in range(2):
-                zz = pull(q, d)
-
-                def hold(zz=zz):
+            if 0 < q < 8:
+                for d in range(2):
+                    zz = pull(q, d)
                     arrived(kb.at[zz], pk_s.at[zz], pk_r.at[zz])
-
-                guard(q > 0 if d == 0 or not isinstance(q, int) else 0 < q < 8, hold)
+            if q == 8:
+                for n, part in enumerate(last_keys):
+                    arrived(part, pk_s.at[NZ + 4 + n], pk_r.at[NZ + 4 + n])
 
             def hold_own():
                 for n, part in enumerate(own_keys):
@@ -388,15 +402,15 @@
         make_gate()
         for load in (loads[2], loads[3], loads[5], loads[6]):
             load.wait()
-        vz_wait(far, cols[0], 8, 0, 0)
-        vz_wait(far, cols[1], 8, 1, 1)
-        vz_wait(far, cols[2], 8, 2, 0)
-        vz_wait(far, cols[3], 8, 3, 1)
-        p_send(far)
+        for n, part in enumerate(last_values):
+            vz_wait(far, cols[n], 8, n, n % 2)
+            send(part, pv_s.at[NZ + 3 + n], pv_r.at[NZ + 3 + n], partner)
         for n, part in enumerate(own_values):
             left(part, pv_s.at[NZ + n], pv_r.at[NZ + n])
-        for step in range(6, 9):
+        for step in range(6, 8):
             pv_left(step)
+        for n, part in enumerate(last_values):
+            left(part, pv_s.at[NZ + 3 + n], pv_r.at[NZ + 3 + n])
         vz_left(7)
         vz_left(8)
         for q in range(9):
@@ -564,8 +578,8 @@
             dma((2, 9, 4)), dma((2, 9, 4)),
             dma((3,)), dma((3,)),
             dma((NZ, 3, 2)), dma((NZ, 3, 2)),
-            dma((NZ + 4,)), dma((NZ + 4,)),
-            dma((NZ + 3,)), dma((NZ + 3,)),
+            dma((NZ + 8,)), dma((NZ + 8,)),
+            dma((NZ + 7,)), dma((NZ + 7,)),
         ],
         compiler_params=pltpu.CompilerParams(
             collective_id=0, has_side_effects=True, vmem_limit_bytes=50 * 1024 * 1024

time: 64.2 us -> 64.1 us (level)
  no operation moved by 1% of the time
where the time goes in v4:
time: 64.1 us; the launch traced here: 63.9 us
  Pallas kernels  63.9 us (100%)
    pallas_call x1, Pallas kernels, local(): pl.pallas_call(gather_body, out_shape=[pltpu.VMEM((NZ, NX, KROWS, 128), B...  57.2 us
    pallas_call x1, Pallas kernels, local(): pl.pallas_call(mix_body, out_shape=jax.ShapeDtypeStruct((ROWS, HEADS * DV...  6.74 us

profile of v4, /device:TPU:1, one launch (start us, length us, event | category | flops | bytes accessed | tf_op | source)
XLA Modules:
  0.0 63.9 jit_solution(4141046357801150177)
XLA Ops:
  0.0 57.2 %gather_rows.1 = (bf16[16,4,432,128]{3,2,1,0:T(8,128)(2,1)S(1)}, bf16[16,4,2,128,128]{4,3,2,1,0:T(8,128)(2,1)S(1)}, bf16[128,2688]{1,0:T(8,128)(2,1)S(1)}, f32[128,32]{1,0:T(8,128)S(1)}, s32[2,16]{1,0:T(2,128)S(4)}) custom-call(bf16[128,2688]{1,0:T(8,128)(2,1)} %q_any.1, bf16[192,128]{1,0:T(8,128)(2,1)} %bitcast.2, bf16[128,128]{1,0:T(8,128)(2,1)} %v_any.1, ...), custom_call_target="tpu_custom_call" | custom-call | tf_op jit(solution)/shard_map/gather_rows/pallas_call | solution.py:556
  57.2 6.7 %attend_mix.1 = bf16[128,1792]{1,0:T(8,128)(2,1)} custom-call(bf16[128,2688]{1,0:T(8,128)(2,1)S(1)} %get-tuple-element.10.q_vm, bf16[16,4,432,128]{3,2,1,0:T(8,128)(2,1)S(1)} %get-tuple-element.11.kb, bf16[16,4,2,128,128]{4,3,2,1,0:T(8,128)(2,1)S(1)} %get-tuple-element.12.vb, f32[128,32]{1,0:T(8,128)S(1)} %get-tuple-element.13.gate_ref, ...), custom_call_target="tpu_custom_call" | custom-call | tf_op jit(solution)/shard_map/attend_mix/pallas_call | solution.py:589
